TPU v7x, 256 devices: a whole 4x4x8 slice. The times are simulated.
256 devices in a mesh: section: 8 (over x, core), fsdp: 32 (over y, z).
Axes of the slice: x: 4, y: 4, z: 8, core: 2. Of those that a mesh axis runs over, the one named last changes fastest.
Arguments:
- tokens: bfloat16 [8, 2, 4096, 8192], P('section', None, 'fsdp'), may hold values from -6 to 6
- queries: bfloat16 [8, 2, 4096, 4096], P('section', None, 'fsdp'), may hold values from -200 to 200
- gains: bfloat16 [8, 8192], P('section'), may hold values from 0.5 to 1.5
- key_weight: bfloat16 [8, 8192, 512], P('section', 'fsdp'), may hold values from -0.0625 to 0.0625
- value_weight: bfloat16 [8, 8192, 512], P('section', 'fsdp'), may hold values from -0.0625 to 0.0625
- lengths: int32 [2, 64], replicated, may hold values from 1 to 128, 4096 in all within a row
Outputs:
- attended: bfloat16 [8, 2, 4096, 4096], P('section', None, 'fsdp')
Inputs may be any that keep to these rules, and one draw needn't show every extreme that they name: `lengths`: each row sums to 4096; some document has exactly 128 tokens.
All inputs are finite; a program needn't handle non-finite values.
Results may differ from a plain program's by a relative error of at most 0.012.
The roundings to bfloat16 on the way count: a program that leaves them out, or rounds other values in their place, can miss the bound.
Values may be sent and summed in bfloat16 or wider, within the bound.
A program may use at most 128 MiB of HBM per device.

v0:
```python
import jax
import jax.numpy as jnp
from jax import lax
from jax.sharding import PartitionSpec as P

HEAD = 128


def side_by_side(arrays, axis, dim, along):
    both = jnp.concatenate(arrays, axis=along)
    out, at, finished = (lax.all_gather(both, axis, axis=dim, tiled=True), 0, [])
    for a in arrays:
        finished.append(lax.slice_in_dim(out, at, at + a.shape[along], axis=along))
        at += a.shape[along]
    return tuple(finished)


def passed_along(block, axis, distance):
    devices = range(lax.axis_size(axis))
    route = [(i - distance, i) for i in devices if i - distance in devices]
    return lax.ppermute(block, axis, route)


def rms_norm(hidden, gain_row):
    widened = hidden.astype(jnp.float32)
    inverse_rms = lax.rsqrt(jnp.mean(widened * widened, axis=-1, keepdims=True) + 1e-05)
    return (widened * inverse_rms * gain_row.astype(jnp.float32)).astype(jnp.bfloat16)


def document_ids(length_row, positions):
    bounds = jnp.cumsum(length_row)
    return jnp.sum((bounds[None, :] <= positions[:, None]).astype(jnp.int32), axis=1)


def block_attend(query_rows, key_rows, value_rows, query_pos, key_pos, query_doc, key_doc):
    query_count = query_rows.shape[0]
    key_count = key_rows.shape[0]
    kv_count = key_rows.shape[1] // HEAD
    group_count = query_rows.shape[1] // (kv_count * HEAD)
    query_heads = query_rows.reshape(query_count, kv_count, group_count, HEAD)
    key_heads = key_rows.reshape(key_count, kv_count, HEAD)
    value_heads = value_rows.reshape(key_count, kv_count, HEAD)
    scores = jnp.einsum(
        "tkgd,skd->kgts", query_heads, key_heads, preferred_element_type=jnp.float32
    ) * HEAD ** (-0.5)
    allowed = (
        (key_doc[None, :] == query_doc[:, None])
        & (key_pos[None, :] <= query_pos[:, None])
        & (key_pos[None, :] >= 0)
    )
    scores = jnp.where(allowed, scores, -1e30)
    maxima = jnp.max(scores, axis=-1, keepdims=True)
    exponent = jnp.where(allowed, jnp.exp(scores - maxima), 0.0)
    totals = jnp.sum(exponent, axis=-1, keepdims=True)
    softmax_rows = (exponent / totals).astype(jnp.bfloat16)
    mixed = jnp.einsum(
        "kgts,skd->tkgd", softmax_rows, value_heads, preferred_element_type=jnp.float32
    )
    return mixed.reshape(query_count, kv_count * group_count * HEAD).astype(jnp.bfloat16)


def body(tokens, queries, gains, key_weight, value_weight, lengths):
    slot_count = tokens.shape[1]
    tok_count = tokens.shape[2]
    key_width = key_weight.shape[2]
    normed = rms_norm(tokens[0], gains[0])
    flat_rows = normed.reshape(slot_count * tok_count, normed.shape[2])

    def add_rows(weight_piece):
        return jnp.dot(flat_rows, weight_piece, preferred_element_type=jnp.float32)

    pieces = side_by_side((key_weight[0], value_weight[0]), "fsdp", 0, 1)
    key_sums = add_rows(pieces[0])
    value_sums = add_rows(pieces[1])
    own_keys = key_sums.astype(jnp.bfloat16).reshape(slot_count, tok_count, key_width)
    own_values = value_sums.astype(jnp.bfloat16).reshape(slot_count, tok_count, key_width)
    prior_keys, prior_values = passed_along((own_keys, own_values), "fsdp", 1)
    all_keys = jnp.concatenate([prior_keys, own_keys], axis=1)
    all_values = jnp.concatenate([prior_values, own_values], axis=1)
    fsdp_index = lax.axis_index("fsdp")
    query_pos = fsdp_index * tok_count + jnp.arange(tok_count, dtype=jnp.int32)
    key_pos = fsdp_index * tok_count - tok_count + jnp.arange(2 * tok_count, dtype=jnp.int32)
    outputs = []
    for slot_index in range(slot_count):
        outputs.append(
            block_attend(
                queries[0, slot_index],
                all_keys[slot_index],
                all_values[slot_index],
                query_pos,
                key_pos,
                document_ids(lengths[slot_index], query_pos),
                document_ids(lengths[slot_index], key_pos),
            )
        )
    return jnp.stack(outputs)[None]


def solution(mesh):
    return jax.shard_map(
        body,
        mesh=mesh,
        in_specs=(
            P("section", None, "fsdp", None),
            P("section", None, "fsdp", None),
            P("section", None),
            P("section", "fsdp", None),
            P("section", "fsdp", None),
            P(),
        ),
        out_specs=P("section", None, "fsdp", None),
        check_vma=False,
    )
```

profile of v0, /device:TPU:16, one launch (start us, length us, event | category | flops | bytes accessed | tf_op | source)
XLA Modules:
  0.0 201.8 jit_solution(9059581040976685564)
XLA Ops:
  6.5 1.9 pad_maximum_fusion
  8.4 0.8 convert_element_type.101
  9.2 0.8 slice_bitcast_fusion
  10.6 1.7 fusion.38
  12.3 0.7 copy.60
  13.0 0.7 copy.59
  13.9 3.3 %multiply_reduce_fusion = f32[2,128]{1,0:T(2,128)S(1)} fusion(bf16[1,2,128,8192]{3,2,1,0:T(8,128)(2,1)} %param.6), kind=kLoop, calls=%fused_computation.9 | loop fusion | flops 6291200 | bytes 4195328 | tf_op jit(solution)/shard_map/reduce_sum | solution.py:26
  17.2 3.1 %fusion.7 = bf16[256,8192]{1,0:T(8,128)(2,1)} fusion(f32[8192]{0:T(1024)S(1)} %bitcast.94, f32[256]{0:T(256)S(1)} %rsqrt_bitcast_fusion, bf16[1,2,128,8192]{3,2,1,0:T(8,128)(2,1)S(1)} %copy-done), kind=kLoop, calls=%fused_computation.8 | loop fusion | flops 8388608 | bytes 8422400 | tf_op jit(solution)/shard_map/convert_element_type | solution.py:27
  20.3 130.6 %all-gather.2.cloned.1.call-done = bf16[8192,1024]{1,0:T(8,128)(2,1)} async-done(((bf16[256,1024]{1,0:T(8,128)(2,1)}), bf16[8192,1024]{1,0:T(8,128)(2,1)}) %all-gather.2.cloned.1.call-update) | async-done | bytes 16777232 | tf_op jit(solution)/shard_map/all_gather | solution.py:11
  150.9 7.1 %fusion.20 = bf16[256,512]{1,0:T(8,128)(2,1)S(1)} fusion(bf16[256,8192]{1,0:T(8,128)(2,1)} %fusion.7, bf16[8192,1024]{1,0:T(8,128)(2,1)} %all-gather.2.cloned.1.call-done), kind=kOutput, calls=%fused_computation.29 | convolution fusion | flops 2147614720 | bytes 12845056 | tf_op jit(solution)/shard_map/dot_general | solution.py:70
  158.0 1.9 collective-permute-start
  160.0 5.7 %fusion.23 = bf16[256,512]{1,0:T(8,128)(2,1)S(1)} fusion(bf16[256,8192]{1,0:T(8,128)(2,1)S(1)} %copy-done.1, bf16[8192,1024]{1,0:T(8,128)(2,1)} %all-gather.2.cloned.1.call-done), kind=kOutput, calls=%fused_computation.30 | convolution fusion | flops 2147614720 | bytes 12845056 | tf_op jit(solution)/shard_map/dot_general | solution.py:70
  165.9 3.2 %collective-permute-start.1 = (bf16[2,128,512]{1,2,0:T(8,128)(2,1)S(1)}, bf16[2,128,512]{1,2,0:T(8,128)(2,1)S(1)}, u32[]{:S(2)}, u32[]{:S(2)}) collective-permute-start(bf16[2,128,512]{1,2,0:T(8,128)(2,1)S(1)} %copy.33), channel_id=1, source_target_pairs={{0,1},{1,2},{2,3},{3,4},{4,5},{5,6},{6,7},{7,8},{8,9},{9,10},{10,1... | collective-permute-start | bytes 786440 | tf_op jit(solution)/shard_map/ppermute | solution.py:21
  169.5 1.0 fusion.31
  170.6 6.6 %collective-permute-done.1 = bf16[2,128,512]{1,2,0:T(8,128)(2,1)S(1)} collective-permute-done((bf16[2,128,512]{1,2,0:T(8,128)(2,1)S(1)}, bf16[2,128,512]{1,2,0:T(8,128)(2,1)S(1)}, u32[]{:S(2)}, u32[]{:S(2)}) %collective-permute-start.1) | collective-permute-done | bytes 262176 | tf_op jit(solution)/shard_map/ppermute | solution.py:21
  177.2 0.8 fusion.30
  178.0 3.6 %fusion.39 = (f32[4,8,128]{2,1,0:T(8,128)S(1)}, f32[4,8,128,256]{2,3,1,0:T(8,128)}) fusion(pred[128,256]{0,1:T(8,128)(4,1)S(1)} %get-tuple-element.16, bf16[256,4,128,1]{0,2,3,1:T(8,128)(2,1)S(1)} %bitcast.93, bf16[128,4,8,128]{0,3,2,1:T(8,128)(2,1)S(1)} %bitcast.82), kind=kOutput, calls=%fused_computation.61 | convolution fusion | flops 273678592 | bytes 5554176 | tf_op jit(solution)/shard_map/sub | solution.py:53
  181.6 2.7 %fusion.18 = bf16[4,128,8,128]{3,1,2,0:T(8,128)(2,1)S(1)} fusion(bf16[256,4,128,1]{0,2,3,1:T(8,128)(2,1)S(1)} %bitcast.85, f32[4,8,128,256]{2,3,1,0:T(8,128)} %get-tuple-element.20, f32[4,8,128]{2,1,0:T(8,128)S(1)} %get-tuple-element.19), kind=kOutput, calls=%fused_computation.27 | convolution fusion | flops 271056896 | bytes 5521408 | tf_op jit(solution)/shard_map/kgts,skd->tkgd/dot_general | solution.py:56
  184.3 0.5 copy.46
  184.8 0.8 copy.31
  185.6 4.6 %fusion.40 = (f32[4,8,128]{2,1,0:T(8,128)S(1)}, f32[4,8,128,256]{2,3,1,0:T(8,128)}) fusion(pred[128,256]{0,1:T(8,128)(4,1)S(1)} %get-tuple-element.15, bf16[256,4,128,1]{0,2,3,1:T(8,128)(2,1)} %bitcast.92, bf16[128,4,8,128]{0,3,2,1:T(8,128)(2,1)S(1)} %bitcast.81), kind=kOutput, calls=%fused_computation.62 | convolution fusion | flops 273678592 | bytes 5554176 | tf_op jit(solution)/shard_map/sub | solution.py:53
  190.2 2.7 %fusion.19 = bf16[4,128,8,128]{3,1,2,0:T(8,128)(2,1)S(1)} fusion(bf16[256,4,128,1]{0,2,3,1:T(8,128)(2,1)S(1)} %bitcast.86, f32[4,8,128,256]{2,3,1,0:T(8,128)} %get-tuple-element.22, f32[4,8,128]{2,1,0:T(8,128)S(1)} %get-tuple-element.21), kind=kOutput, calls=%fused_computation.28 | convolution fusion | flops 271056896 | bytes 5521408 | tf_op jit(solution)/shard_map/kgts,skd->tkgd/dot_general | solution.py:56
  192.9 0.5 copy.45
  193.5 1.5 maximum_bitcast_fusion
  (24 shorter events, 1.5 us)
Async XLA Ops:
  6.5 144.4 %all-gather.2.cloned.1.call-start = ((), (), s32[]{:S(2)}) async-start(), calls=%async_computation | async-start | bytes 17301504 | tf_op jit(solution)/shard_map/all_gather | solution.py:11
  13.6 3.5 %copy-start = (bf16[1,2,128,8192]{3,2,1,0:T(8,128)(2,1)S(1)}, bf16[1,2,128,8192]{3,2,1,0:T(8,128)(2,1)}, u32[]{:S(2)}) copy-start(bf16[1,2,128,8192]{3,2,1,0:T(8,128)(2,1)} %param.6) | copy-start | bytes 12582916
  150.9 9.1 %copy-start.1 = (bf16[256,8192]{1,0:T(8,128)(2,1)S(1)}, bf16[256,8192]{1,0:T(8,128)(2,1)}, u32[]{:S(2)}) copy-start(bf16[256,8192]{1,0:T(8,128)(2,1)} %fusion.7) | copy-start | bytes 12582916
  158.0 11.4 %collective-permute-start = (bf16[2,128,512]{2,1,0:T(8,128)(2,1)S(1)}, bf16[2,128,512]{2,1,0:T(8,128)(2,1)}, u32[]{:S(2)}, u32[]{:S(2)}) collective-permute-start(bf16[2,128,512]{2,1,0:T(8,128)(2,1)S(1)} %bitcast.90), channel_id=1, source_target_pairs={{0,1},{1,2},{2,3},{3,4},{4,5},{5,6},{6,7},{7,8},{8,9},{9,10},{10,1... | collective-permute-start | bytes 786440 | tf_op jit(solution)/shard_map/ppermute | solution.py:21
  165.9 11.3 %collective-permute-start.1 = (bf16[2,128,512]{1,2,0:T(8,128)(2,1)S(1)}, bf16[2,128,512]{1,2,0:T(8,128)(2,1)S(1)}, u32[]{:S(2)}, u32[]{:S(2)}) collective-permute-start(bf16[2,128,512]{1,2,0:T(8,128)(2,1)S(1)} %copy.33), channel_id=1, source_target_pairs={{0,1},{1,2},{2,3},{3,4},{4,5},{5,6},{6,7},{7,8},{8,9},{9,10},{10,1... | collective-permute-start | bytes 786440 | tf_op jit(solution)/shard_map/ppermute | solution.py:21
  185.6 4.6 %copy-start.2 = (bf16[1,256,512]{1,2,0:T(8,128)(2,1)S(1)}, bf16[1,256,512]{1,2,0:T(8,128)(2,1)}, u32[]{:S(2)}) copy-start(bf16[1,256,512]{1,2,0:T(8,128)(2,1)} %copy.31) | copy-start | bytes 786436
Sparse Core Ops, SparseCore 0:
  9.9 140.9 all-gather.1
where the time goes:
time: 203 us; the launch traced here: 202 us
  waiting for transfers between devices  137 us (67%)
  matrix products  26.4 us (13%)
  between operations  13.6 us (7%)
  other arithmetic  13.1 us (6%)
  local copies, waits for them, and re-layouts  6.17 us (3%)
  starting transfers between devices  5.17 us (3%)
    all_gather x1, waiting for transfers between devices, side_by_side(): lax.all_gather(both, axis, axis=dim, tiled=True)  131 us
    dot_general x2, matrix products, add_rows(): return jnp.dot(flat_rows, weight_piece, preferred_element_type=jnp.float32)  12.9 us
    sub x2, matrix products, block_attend(): exponent = jnp.where(allowed, jnp.exp(scores - maxima), 0.0)  8.17 us
    ppermute x2, waiting for transfers between devices, passed_along(): return lax.ppermute(block, axis, route)  6.72 us
    dot_general x2, matrix products, block_attend(): jnp.einsum('kgts,skd->tkgd', softmax_rows, value_heads, preferred_element...  5.4 us
    ppermute x2, starting transfers between devices, passed_along(): return lax.ppermute(block, axis, route)  5.16 us
  transfers between devices with their start and end apart: 3, of which 3 were waited for; matrix products, arithmetic and copies ran while one was open for 9% of the time, Pallas kernels for 0%

commit v1 on v0

v1 whole, which is shorter than its diff:
```python
import functools

import jax
import jax.numpy as jnp
from jax import lax
from jax.experimental import pallas as pl
from jax.experimental.pallas import tpu as pltpu
from jax.sharding import PartitionSpec as P

HEAD = 128
GROUPS = 4
FAN = 8
MICRO = 2
TOK = 128
ROWS = 256
BLOCKS = 16
HALF = ROWS * BLOCKS
WIDE = 2 * HEAD
DOCS = 64
XCUT = 4
MESH = pl.DeviceIdType.MESH

FORWARD = ((0, 0), (0, 1), (0, 2), (0, 3), (1, 2))
BACKWARD = ((0, 0), (0, -1), (0, -2), (1, 0), (1, -1))
ACROSS = ((0, 0), (0, 1), (0, 2), (0, -3), (0, 4))


def kernel(
    tok, queries, gains, key_w, value_w, lengths, out,
    wbuf, xown, xoth, xprt, xn, gown, qbuf, obuf, lens, inv_own, inv_send, inv_recv,
    bias, p_own, p_send, p_recv, kv,
    w_send, w_recv, x_send, x_recv, i_send, i_recv, p_ssem, p_rsem, h_send, h_recv, local, o_sem,
):
    me = lax.axis_index("fsdp")
    y, z = me // 8, me % 8
    half, row = y // 2, y % 2
    z_next, z_prev = y * 8 + (z + 1) % 8, y * 8 + (z + 7) % 8
    mate = (y + 1 - 2 * row) * 8 + z
    partner = (3 - y) * 8 + z
    after, before = (me + 1) % 32, (me + 31) % 32

    def block_at(r, d):
        source_row = row if r == 0 else 1 - row
        source_z = (z - d + 8) % 8
        return pl.ds(pl.multiple_of((source_row * 8 + source_z) * ROWS, ROWS), ROWS)

    own_rows = block_at(0, 0)
    own_cols = pl.multiple_of(half * HALF, HALF)
    other_cols = pl.multiple_of((1 - half) * HALF, HALF)

    loads = []
    w_loads = []
    for g in range(GROUPS):
        cols = pl.ds(g * HEAD, HEAD)
        w_loads.append((
            pltpu.make_async_copy(key_w.at[0, :, cols], wbuf.at[g, own_rows, pl.ds(0, HEAD)], local.at[2 * g]),
            pltpu.make_async_copy(value_w.at[0, :, cols], wbuf.at[g, own_rows, pl.ds(HEAD, HEAD)], local.at[2 * g + 1]),
        ))
    for pair in w_loads:
        for c in pair:
            c.start()
    x_other = pltpu.make_async_copy(tok.at[0, :, :, pl.ds(other_cols, HALF)], xoth, local.at[8])
    x_mine = pltpu.make_async_copy(tok.at[0, :, :, pl.ds(own_cols, HALF)], xown, local.at[9])
    g_load = pltpu.make_async_copy(gains.at[:, pl.ds(own_cols, HALF)], gown, local.at[10])
    l_load = pltpu.make_async_copy(lengths, lens, local.at[11])
    q_load = pltpu.make_async_copy(queries.at[0], qbuf, local.at[12])
    for c in (x_other, x_mine, g_load, l_load, q_load):
        c.start()

    barrier = pltpu.get_barrier_semaphore()
    for device in (z_next, z_prev, mate, partner, after, before):
        pl.semaphore_signal(barrier, inc=1, device_id={"fsdp": device}, device_id_type=MESH)
    pl.semaphore_wait(barrier, 6)

    links = ((0, z_next, FORWARD), (1, z_prev, BACKWARD), (2, mate, ACROSS))

    def w_copy(link, g, p, where):
        k, device, _ = links[link]
        return pltpu.make_async_remote_copy(
            src_ref=wbuf.at[g, where],
            dst_ref=wbuf.at[g, where],
            send_sem=w_send.at[k, g, p],
            recv_sem=w_recv.at[k, g, p],
            device_id={"fsdp": device},
            device_id_type=MESH,
        )

    def w_start(g, p):
        for link in (0, 1, 2):
            w_copy(link, g, p, block_at(*links[link][2][p])).start()

    def w_arrive(g, p):
        for link, (dr, dd) in ((0, (0, 1)), (1, (0, -1)), (2, (1, 0))):
            r, d = links[link][2][p]
            w_copy(link, g, p, block_at((r + dr) % 2, d + dd)).wait_recv()

    def w_step(g, p):
        w_arrive(g, p - 1)
        w_start(g, p)

    def x_copy(j):
        width = HALF // XCUT
        return pltpu.make_async_remote_copy(
            src_ref=xoth.at[:, :, pl.ds(j * width, width)],
            dst_ref=xprt.at[:, :, pl.ds(j * width, width)],
            send_sem=x_send.at[j],
            recv_sem=x_recv.at[j],
            device_id={"fsdp": partner},
            device_id_type=MESH,
        )

    def inv_copy():
        return pltpu.make_async_remote_copy(
            src_ref=inv_send, dst_ref=inv_recv, send_sem=i_send, recv_sem=i_recv,
            device_id={"fsdp": partner}, device_id_type=MESH,
        )

    def part_copy(g):
        return pltpu.make_async_remote_copy(
            src_ref=p_send.at[g], dst_ref=p_recv.at[g], send_sem=p_ssem.at[g], recv_sem=p_rsem.at[g],
            device_id={"fsdp": partner}, device_id_type=MESH,
        )

    def halo_copy(g):
        return pltpu.make_async_remote_copy(
            src_ref=kv.at[g, :, pl.ds(TOK, TOK)], dst_ref=kv.at[g, :, pl.ds(0, TOK)],
            send_sem=h_send.at[g], recv_sem=h_recv.at[g],
            device_id={"fsdp": after}, device_id_type=MESH,
        )

    def out_copy(g):
        cols = pl.ds(g * FAN * HEAD, FAN * HEAD)
        return pltpu.make_async_copy(obuf.at[:, :, cols], out.at[0, :, :, cols], o_sem.at[g])

    def eye(n):
        return lax.broadcasted_iota(jnp.int32, (n, n), 0) == lax.broadcasted_iota(jnp.int32, (n, n), 1)

    def squares():
        for m in range(MICRO):
            def add(j, total):
                at = pl.ds(pl.multiple_of(j * 512, 512), 512)
                for x in (xown, xoth):
                    v = x[m, :, at].astype(jnp.float32)
                    v = v * v
                    for i in range(4):
                        total = total + v[:, i * 128:(i + 1) * 128]
                return total
            total = lax.fori_loop(0, HALF // 512, add, jnp.zeros((TOK, 128), jnp.float32))
            mean = jnp.sum(total, axis=1, keepdims=True) * (1.0 / (2 * HALF))
            inverse = jnp.broadcast_to(lax.rsqrt(mean + 1e-05), (TOK, 128))
            inv_own[m] = inverse
            inv_send[m:m + 1, :] = jnp.sum(jnp.where(eye(TOK), inverse, 0.0), axis=0, keepdims=True)

    def normalise(x, base, m, inverse, start, width):
        def one(j, _):
            at = pl.ds(pl.multiple_of(start + j * 256, 256), 256)
            v = x[m, :, at].astype(jnp.float32)
            scaled = v * jnp.concatenate([inverse, inverse], axis=1)
            xn[pl.ds(base + m * TOK, TOK), at] = (scaled * gown[:, at].astype(jnp.float32)).astype(jnp.bfloat16)
            return 0
        lax.fori_loop(0, width // 256, one, 0)

    def normalise_own():
        for m in range(MICRO):
            normalise(xown, 0, m, inv_own[m], 0, HALF)

    def normalise_partner(j):
        for m in range(MICRO):
            line = jnp.broadcast_to(inv_recv[m:m + 1, :], (TOK, TOK))
            column = jnp.sum(jnp.where(eye(TOK), line, 0.0), axis=1, keepdims=True)
            normalise(xprt, 2 * TOK, m, jnp.broadcast_to(column, (TOK, 128)), j * (HALF // XCUT), HALF // XCUT)

    def masks():
        for m in range(MICRO):
            lane = lax.broadcasted_iota(jnp.int32, (DOCS, DOCS), 1)
            sub = lax.broadcasted_iota(jnp.int32, (DOCS, DOCS), 0)
            line = jnp.broadcast_to(lens[m:m + 1, :].astype(jnp.float32), (DOCS, DOCS))
            bound_column = jnp.sum(jnp.where(lane <= sub, line, 0.0), axis=1, keepdims=True)
            column = jnp.sum(jnp.where(lane == sub, line, 0.0), axis=1, keepdims=True)
            bound_line = jnp.sum(jnp.where(sub <= lane, column, 0.0), axis=0, keepdims=True)
            start = me * TOK
            key_pos = (lax.broadcasted_iota(jnp.int32, (DOCS, 2 * TOK), 1) + (start - TOK)).astype(jnp.float32)
            key_doc = jnp.sum(jnp.where(bound_column <= key_pos, 1.0, 0.0), axis=0, keepdims=True)
            query_pos = (lax.broadcasted_iota(jnp.int32, (TOK, DOCS), 0) + start).astype(jnp.float32)
            query_doc = jnp.sum(jnp.where(bound_line <= query_pos, 1.0, 0.0), axis=1, keepdims=True)
            kp = lax.broadcasted_iota(jnp.int32, (TOK, 2 * TOK), 1) + (start - TOK)
            qp = lax.broadcasted_iota(jnp.int32, (TOK, 2 * TOK), 0) + start
            allowed = (key_doc == query_doc) & (kp <= qp) & (kp >= 0)
            bias[m] = jnp.where(allowed, 0.0, -1e30)

    def dot_own(g):
        p_own[g] = jnp.dot(xn[0:2 * TOK, :], wbuf[g], preferred_element_type=jnp.float32)

    def dot_partner(g):
        p_send[g] = jnp.dot(
            xn[2 * TOK:4 * TOK, :], wbuf[g], preferred_element_type=jnp.float32
        ).astype(jnp.bfloat16)

    def finish_kv(g):
        part_copy(g).wait_recv()
        for m in range(MICRO):
            at = pl.ds(m * TOK, TOK)
            kv[g, m, TOK:2 * TOK, :] = (p_own[g, at] + p_recv[g, at].astype(jnp.float32)).astype(jnp.bfloat16)
        halo_copy(g).start()

    def attend(g):
        halo_copy(g).wait_recv()
        factor = HEAD ** (-0.5) * 1.4426950408889634
        for m in range(MICRO):
            keys = kv[g, m, :, 0:HEAD]
            values = kv[g, m, :, HEAD:WIDE]

            def one(j, _):
                at = pl.ds(pl.multiple_of((g * FAN + j) * HEAD, HEAD), HEAD)
                s = lax.dot_general(
                    qbuf[m, :, at], keys, (((1,), (1,)), ((), ())), preferred_element_type=jnp.float32
                ) + bias[m]
                e = jnp.exp2((s - jnp.max(s, axis=1, keepdims=True)) * factor)
                weights = (e * (1.0 / jnp.sum(e, axis=1, keepdims=True))).astype(jnp.bfloat16)
                obuf[m, :, at] = jnp.dot(weights, values, preferred_element_type=jnp.float32).astype(jnp.bfloat16)
                return 0
            lax.fori_loop(0, FAN, one, 0, unroll=True)
        out_copy(g).start()

    for g in (0, 1, 2):
        for c in w_loads[g]:
            c.wait()
        w_start(g, 0)
        if g == 0:
            x_other.wait()
            x_copy(0).start()
    for c in w_loads[3]:
        c.wait()
    x_mine.wait()
    g_load.wait()
    l_load.wait()
    q_load.wait()
    squares()
    inv_copy().start()
    for j in range(1, XCUT):
        x_copy(j).start()
    w_step(0, 1)
    normalise_own()
    w_step(1, 1)
    masks()
    w_step(0, 2)
    w_step(1, 2)
    w_step(0, 3)
    inv_copy().wait_recv()
    x_copy(0).wait_recv()
    normalise_partner(0)
    w_step(1, 3)
    w_step(0, 4)
    w_step(1, 4)
    w_start(3, 0)
    x_copy(1).wait_recv()
    normalise_partner(1)
    w_step(2, 1)
    w_arrive(0, 4)
    dot_own(0)
    w_step(3, 1)
    w_arrive(1, 4)
    dot_own(1)
    w_step(2, 2)
    x_copy(2).wait_recv()
    normalise_partner(2)
    w_step(3, 2)
    w_step(2, 3)
    x_copy(3).wait_recv()
    normalise_partner(3)
    dot_partner(0)
    part_copy(0).start()
    w_step(3, 3)
    dot_partner(1)
    part_copy(1).start()
    w_step(2, 4)
    finish_kv(0)
    w_step(3, 4)
    finish_kv(1)
    w_arrive(2, 4)
    dot_partner(2)
    part_copy(2).start()
    dot_own(2)
    w_arrive(3, 4)
    dot_partner(3)
    part_copy(3).start()
    dot_own(3)
    finish_kv(2)
    attend(0)
    finish_kv(3)
    attend(1)
    attend(2)
    attend(3)

    for g in range(GROUPS):
        for p in range(5):
            for link in (0, 1, 2):
                w_copy(link, g, p, block_at(*links[link][2][p])).wait_send()
    for j in range(XCUT):
        x_copy(j).wait_send()
    inv_copy().wait_send()
    for g in range(GROUPS):
        part_copy(g).wait_send()
        halo_copy(g).wait_send()
        out_copy(g).wait()


def body(tokens, queries, gains, key_weight, value_weight, lengths):
    bf16, f32 = jnp.bfloat16, jnp.float32
    return pl.pallas_call(
        kernel,
        out_shape=jax.ShapeDtypeStruct(queries.shape, bf16),
        in_specs=[pl.BlockSpec(memory_space=pl.ANY)] * 6,
        out_specs=pl.BlockSpec(memory_space=pl.ANY),
        scratch_shapes=[
            pltpu.VMEM((GROUPS, HALF, WIDE), bf16),
            pltpu.VMEM((MICRO, TOK, HALF), bf16),
            pltpu.VMEM((MICRO, TOK, HALF), bf16),
            pltpu.VMEM((MICRO, TOK, HALF), bf16),
            pltpu.VMEM((4 * TOK, HALF), bf16),
            pltpu.VMEM((1, HALF), bf16),
            pltpu.VMEM((MICRO, TOK, GROUPS * FAN * HEAD), bf16),
            pltpu.VMEM((MICRO, TOK, GROUPS * FAN * HEAD), bf16),
            pltpu.VMEM((MICRO, DOCS), jnp.int32),
            pltpu.VMEM((MICRO, TOK, 128), f32),
            pltpu.VMEM((8, 128), f32),
            pltpu.VMEM((8, 128), f32),
            pltpu.VMEM((MICRO, TOK, 2 * TOK), f32),
            pltpu.VMEM((GROUPS, 2 * TOK, WIDE), f32),
            pltpu.VMEM((GROUPS, 2 * TOK, WIDE), bf16),
            pltpu.VMEM((GROUPS, 2 * TOK, WIDE), bf16),
            pltpu.VMEM((GROUPS, MICRO, 2 * TOK, WIDE), bf16),
            pltpu.SemaphoreType.DMA((3, GROUPS, 5)),
            pltpu.SemaphoreType.DMA((3, GROUPS, 5)),
            pltpu.SemaphoreType.DMA((XCUT,)),
            pltpu.SemaphoreType.DMA((XCUT,)),
            pltpu.SemaphoreType.DMA,
            pltpu.SemaphoreType.DMA,
            pltpu.SemaphoreType.DMA((GROUPS,)),
            pltpu.SemaphoreType.DMA((GROUPS,)),
            pltpu.SemaphoreType.DMA((GROUPS,)),
            pltpu.SemaphoreType.DMA((GROUPS,)),
            pltpu.SemaphoreType.DMA((13,)),
            pltpu.SemaphoreType.DMA((GROUPS,)),
        ],
        compiler_params=pltpu.CompilerParams(collective_id=0, has_side_effects=True),
        name="window",
    )(tokens, queries, gains, key_weight, value_weight, lengths)


def solution(mesh):
    return jax.shard_map(
        body,
        mesh=mesh,
        in_specs=(
            P("section", None, "fsdp", None),
            P("section", None, "fsdp", None),
            P("section", None),
            P("section", "fsdp", None),
            P("section", "fsdp", None),
            P(),
        ),
        out_specs=P("section", None, "fsdp", None),
        check_vma=False,
    )
```

time: 203 us -> 92.4 us (0.46)
  waiting for transfers between devices: 137 us -> 0 us
  Pallas kernels: 0 us -> 87.9 us
  matrix products: 26.4 us -> 0 us
  between operations: 13.6 us -> 0.01 us
  other arithmetic: 13.1 us -> 0 us
  starting transfers between devices: 5.17 us -> 0 us
  local copies, waits for them, and re-layouts: 6.17 us -> 3.13 us
    all_gather x1 -> x0, waiting for transfers between devices: 131 us -> none  [side_by_side(): lax.all_gather(both, axis, axis=dim, tiled=True)]
    pallas_call x0 -> x1, Pallas kernels: none -> 87.9 us  [body(): pl.pallas_call(kernel, out_shape=jax.ShapeDtypeStruct(queries.shape, bf16...]
    dot_general x4 -> x0, matrix products: 18.3 us -> none  [the longest x2 12.9 us: add_rows(): return jnp.dot(flat_rows, weight_piece, preferred_element_type=jnp.float32)]
    sub x2 -> x0, matrix products: 8.17 us -> none  [block_attend(): exponent = jnp.where(allowed, jnp.exp(scores - maxima), 0.0)]
    ppermute x2 -> x0, waiting for transfers between devices: 6.72 us -> none  [passed_along(): return lax.ppermute(block, axis, route)]
    ppermute x2 -> x0, starting transfers between devices: 5.16 us -> none  [passed_along(): return lax.ppermute(block, axis, route)]
    convert_element_type x2 -> x0, other arithmetic: 3.91 us -> none  [the longest x1 3.11 us: rms_norm(): (widened * inverse_rms * gain_row.astype(jnp.float32)).astype(jnp.bfloat16)]
    concatenate x3 -> x0, other arithmetic: 3.64 us -> none  [the longest x1 1.87 us: side_by_side(): both = jnp.concatenate(arrays, axis=along)]
  transfers between devices with their start and end apart: 3 -> 0, of which waited for: 3 -> 0; matrix products, arithmetic and copies ran while one was open for 9% -> 0% of each run, Pallas kernels for 0% -> 0%
where the time goes in v1:
time: 92.4 us; the launch traced here: 91.1 us
  Pallas kernels  87.9 us (95%)
  local copies, waits for them, and re-layouts  3.13 us (3%)
    pallas_call x1, Pallas kernels, body(): pl.pallas_call(kernel, out_shape=jax.ShapeDtypeStruct(queries.shape, bf16...  87.9 us
    unnamed x1, local copies, waits for them, and re-layouts  3.13 us

profile of v1, /device:TPU:16, one launch (start us, length us, event | category | flops | bytes accessed | tf_op | source)
XLA Modules:
  0.0 91.1 jit_solution(10485524535621913546)
XLA Ops:
  0.0 87.9 %window.1 = bf16[1,2,128,4096]{3,2,1,0:T(8,128)(2,1)} custom-call(bf16[1,2,128,8192]{3,2,1,0:T(8,128)(2,1)} %tok.1, bf16[1,2,128,4096]{3,2,1,0:T(8,128)(2,1)} %queries.1, bf16[1,8192]{1,0:T(2,128)(2,1)} %gains.1, bf16[1,256,512]{2,1,0:T(8,128)(2,1)} %key_w.1, bf16[1,256,512]{2,1,0:T(8,128)(2,1)} %value_w.1, s32[2,64]{1,0:T(2,128)} %lengths.1), custom_call_target="tpu_custom_call" | custom-call | tf_op jit(solution)/shard_map/window/pallas_call | solution.py:310
  87.9 3.1 %copy.8 = bf16[1,2,128,4096]{3,2,1,0:T(8,128)(2,1)} copy(bf16[1,2,128,4096]{3,2,1,0:T(8,128)(2,1)} %window.1) | data formatting | bytes 4194304

commit v2 on v1

--- a/solution.py
+++ b/solution.py
@@ -20,16 +20,40 @@
 XCUT = 4
 MESH = pl.DeviceIdType.MESH
 
-FORWARD = ((0, 0), (0, 1), (0, 2), (0, 3), (1, 2))
-BACKWARD = ((0, 0), (0, -1), (0, -2), (1, 0), (1, -1))
-ACROSS = ((0, 0), (0, 1), (0, 2), (0, -3), (0, 4))
+EVEN = (
+    (((0, 0),), ((0, 1),), ((0, 2),), ((0, 3),), ((1, 2),)),
+    (((0, 0),), ((0, -1),), ((0, -2),), ((1, 0),), ((1, -1),)),
+    (((0, 0),), ((0, 1),), ((0, 2),), ((0, -3),), ((0, 4),)),
+)
+BACK = (
+    (((0, 0),), ((0, 1),), ((0, 2),), ((1, 2),), ()),
+    (((0, 0),), ((0, -1),), ((0, -2), (1, 0)), ((0, -3),), ((1, -1),)),
+    (((0, 0),), ((0, 1),), ((0, 2),), ((0, -3),), ((0, -4),)),
+)
+SIDE = (
+    (((0, 0),), ((0, 1),), ((0, 2),), ((0, 3),), ()),
+    (((0, 0),), ((0, -1),), ((0, -2),), ((1, 0),), ((1, -1),)),
+    (((0, 0),), ((0, 1),), ((0, 2),), ((0, 3), (0, -3)), ((0, 4),)),
+)
+PATTERN = (EVEN, EVEN, BACK, SIDE)
+MOVES = ((0, 1), (0, -1), (1, 0))
+SENDS = [[[(p, item) for p, items in enumerate(link) for item in items] for link in pattern] for pattern in PATTERN]
+ARRIVALS = [
+    {
+        ((r + MOVES[k][0]) % 2, d + MOVES[k][1]): (k, i)
+        for k, link in enumerate(links)
+        for i, (_, (r, d)) in enumerate(link)
+    }
+    for links in SENDS
+]
+LATE = ((), (), ((1, 3), (1, 4), (2, 4)), ((1, 3), (1, 4), (2, 3), (2, 4)))
 
 
 def kernel(
     tok, queries, gains, key_w, value_w, lengths, out,
-    wbuf, xown, xoth, xprt, xn, gown, qbuf, obuf, lens, inv_own, inv_send, inv_recv,
-    bias, p_own, p_send, p_recv, kv,
-    w_send, w_recv, x_send, x_recv, i_send, i_recv, p_ssem, p_rsem, h_send, h_recv, local, o_sem,
+    wbuf, xown, xoth, xprt, xn, gown, qbuf, lens, inv_own, inv_send, inv_recv,
+    bias, acc, p_own, p_send, p_recv, kv, passing,
+    w_send, w_recv, x_send, x_recv, i_send, i_recv, p_ssem, p_rsem, h_send, h_recv, r_send, r_recv, local,
 ):
     me = lax.axis_index("fsdp")
     y, z = me // 8, me % 8
@@ -37,6 +61,7 @@
     z_next, z_prev = y * 8 + (z + 1) % 8, y * 8 + (z + 7) % 8
     mate = (y + 1 - 2 * row) * 8 + z
     partner = (3 - y) * 8 + z
+    below = jnp.minimum(me + 8, 31)
     after, before = (me + 1) % 32, (me + 31) % 32
 
     def block_at(r, d):
@@ -67,36 +92,55 @@
     for c in (x_other, x_mine, g_load, l_load, q_load):
         c.start()
 
+    @pl.when(me == 0)
+    def _():
+        for g in range(GROUPS):
+            kv[g, :, 0:TOK, :] = jnp.zeros((MICRO, TOK, WIDE), jnp.bfloat16)
+
     barrier = pltpu.get_barrier_semaphore()
     for device in (z_next, z_prev, mate, partner, after, before):
         pl.semaphore_signal(barrier, inc=1, device_id={"fsdp": device}, device_id_type=MESH)
-    pl.semaphore_wait(barrier, 6)
-
-    links = ((0, z_next, FORWARD), (1, z_prev, BACKWARD), (2, mate, ACROSS))
-
-    def w_copy(link, g, p, where):
-        k, device, _ = links[link]
+    def barrier_wait():
+        pl.semaphore_wait(barrier, 6)
+
+    barrier_wait()
+
+    targets = (z_next, z_prev, mate)
+    here = [{(0, 0)} for _ in range(GROUPS)]
+
+    def w_copy(g, k, i, where):
         return pltpu.make_async_remote_copy(
             src_ref=wbuf.at[g, where],
             dst_ref=wbuf.at[g, where],
-            send_sem=w_send.at[k, g, p],
-            recv_sem=w_recv.at[k, g, p],
-            device_id={"fsdp": device},
+            send_sem=w_send.at[k, g, i],
+            recv_sem=w_recv.at[k, g, i],
+            device_id={"fsdp": targets[k]},
             device_id_type=MESH,
         )
 
-    def w_start(g, p):
-        for link in (0, 1, 2):
-            w_copy(link, g, p, block_at(*links[link][2][p])).start()
-
-    def w_arrive(g, p):
-        for link, (dr, dd) in ((0, (0, 1)), (1, (0, -1)), (2, (1, 0))):
-            r, d = links[link][2][p]
-            w_copy(link, g, p, block_at((r + dr) % 2, d + dd)).wait_recv()
-
-    def w_step(g, p):
-        w_arrive(g, p - 1)
-        w_start(g, p)
+    def w_need(g, item):
+        if item not in here[g]:
+            here[g].add(item)
+            w_copy(g, *ARRIVALS[g][item], block_at(*item)).wait_recv()
+
+    def w_step(g, p, links=(0, 1, 2), at=None):
+        for k in links:
+            for i, (position, item) in enumerate(SENDS[g][k]):
+                if position == p and at in (None, item):
+                    w_need(g, item)
+                    w_copy(g, k, i, block_at(*item)).start()
+
+    def w_late(g):
+        return [item for item, (k, i) in ARRIVALS[g].items() if (k, SENDS[g][k][i][0]) in LATE[g] and not (
+            g == 3 and k == 2 and SENDS[g][k][i][1] == (0, 3))]
+
+    def w_early(g):
+        late = w_late(g)
+        return [(0, 0)] + [item for item in ARRIVALS[g] if item not in late]
+
+    def w_rest(g, items):
+        for item in items:
+            w_need(g, item)
 
     def x_copy(j):
         width = HALF // XCUT
@@ -115,22 +159,55 @@
             device_id={"fsdp": partner}, device_id_type=MESH,
         )
 
-    def part_copy(g):
+    def part_copy(g, m):
+        at = pl.ds(m * TOK, TOK)
         return pltpu.make_async_remote_copy(
-            src_ref=p_send.at[g], dst_ref=p_recv.at[g], send_sem=p_ssem.at[g], recv_sem=p_rsem.at[g],
+            src_ref=p_send.at[g, at], dst_ref=p_recv.at[g, at],
+            send_sem=p_ssem.at[g, m], recv_sem=p_rsem.at[g, m],
             device_id={"fsdp": partner}, device_id_type=MESH,
         )
 
-    def halo_copy(g):
+    def halo_to(g, m, device, into=None):
         return pltpu.make_async_remote_copy(
-            src_ref=kv.at[g, :, pl.ds(TOK, TOK)], dst_ref=kv.at[g, :, pl.ds(0, TOK)],
-            send_sem=h_send.at[g], recv_sem=h_recv.at[g],
-            device_id={"fsdp": after}, device_id_type=MESH,
+            src_ref=kv.at[g, m, pl.ds(TOK, TOK)],
+            dst_ref=kv.at[g, m, pl.ds(0, TOK)] if into is None else into,
+            send_sem=h_send.at[g, m],
+            recv_sem=(h_recv.at[g, m] if into is None else r_recv.at[g]),
+            device_id={"fsdp": device}, device_id_type=MESH,
         )
 
-    def out_copy(g):
-        cols = pl.ds(g * FAN * HEAD, FAN * HEAD)
-        return pltpu.make_async_copy(obuf.at[:, :, cols], out.at[0, :, :, cols], o_sem.at[g])
+    def pass_on(g, m, device):
+        return pltpu.make_async_remote_copy(
+            src_ref=passing.at[g], dst_ref=kv.at[g, m, pl.ds(0, TOK)],
+            send_sem=r_send.at[g], recv_sem=h_recv.at[g, m],
+            device_id={"fsdp": device}, device_id_type=MESH,
+        )
+
+    def halo_start(g, m):
+        @pl.when(z < 7)
+        def _():
+            halo_to(g, m, z_next).start()
+
+        if g < 2:
+            @pl.when((z == 7) & (y < 3))
+            def _():
+                halo_to(g, m, z_next if m == 1 else below, passing.at[g]).start()
+        else:
+            @pl.when((z == 7) & (y < 3))
+            def _():
+                halo_to(g, m, after).start()
+
+    def relay(g):
+        if g < 2:
+            @pl.when((z == 0) & (y < 3))
+            def _():
+                halo_to(g, 1, z_next, passing.at[g]).wait_recv()
+                pass_on(g, 1, below).start()
+
+            @pl.when((z == 7) & (y > 0))
+            def _():
+                halo_to(g, 0, z_next, passing.at[g]).wait_recv()
+                pass_on(g, 0, z_next).start()
 
     def eye(n):
         return lax.broadcasted_iota(jnp.int32, (n, n), 0) == lax.broadcasted_iota(jnp.int32, (n, n), 1)
@@ -195,46 +272,81 @@
         p_send[g] = jnp.dot(
             xn[2 * TOK:4 * TOK, :], wbuf[g], preferred_element_type=jnp.float32
         ).astype(jnp.bfloat16)
-
-    def finish_kv(g):
-        part_copy(g).wait_recv()
-        for m in range(MICRO):
-            at = pl.ds(m * TOK, TOK)
-            kv[g, m, TOK:2 * TOK, :] = (p_own[g, at] + p_recv[g, at].astype(jnp.float32)).astype(jnp.bfloat16)
-        halo_copy(g).start()
-
-    def attend(g):
-        halo_copy(g).wait_recv()
+        for m in range(MICRO):
+            part_copy(g, m).start()
+
+    def add_blocks(total, g, items, first, count):
+        for item in items:
+            at = block_at(*item)
+            total = total + jnp.dot(
+                xn[first:first + count, at], wbuf[g, at, :], preferred_element_type=jnp.float32
+            )
+        return total
+
+    def dot_early(g):
+        for first in (0, 2 * TOK):
+            acc[g - 2, first:first + 2 * TOK] = add_blocks(
+                jnp.zeros((2 * TOK, WIDE), jnp.float32), g, w_early(g), first, 2 * TOK
+            )
+
+    def dot_late(g):
+        for m in range(MICRO):
+            first = (2 + m) * TOK
+            p_send[g, m * TOK:(m + 1) * TOK] = add_blocks(
+                acc[g - 2, first:first + TOK], g, w_late(g), first, TOK
+            ).astype(jnp.bfloat16)
+            part_copy(g, m).start()
+        p_own[g] = add_blocks(acc[g - 2, 0:2 * TOK], g, w_late(g), 0, 2 * TOK)
+
+    def part_wait(g, m):
+        part_copy(g, m).wait_recv()
+
+    def halo_wait(g, m):
+        @pl.when(me > 0)
+        def _():
+            halo_to(g, m, z_next).wait_recv()
+
+    def x_wait(j):
+        x_copy(j).wait_recv()
+
+    def inv_wait():
+        inv_copy().wait_recv()
+
+    def start_wait():
+        for c in (x_mine, g_load, l_load, q_load):
+            c.wait()
+
+    def finish_kv(g, m):
+        at = pl.ds(m * TOK, TOK)
+        kv[g, m, TOK:2 * TOK, :] = (p_own[g, at] + p_recv[g, at].astype(jnp.float32)).astype(jnp.bfloat16)
+        halo_start(g, m)
+
+    def attend(g, m):
         factor = HEAD ** (-0.5) * 1.4426950408889634
-        for m in range(MICRO):
-            keys = kv[g, m, :, 0:HEAD]
-            values = kv[g, m, :, HEAD:WIDE]
-
-            def one(j, _):
-                at = pl.ds(pl.multiple_of((g * FAN + j) * HEAD, HEAD), HEAD)
-                s = lax.dot_general(
-                    qbuf[m, :, at], keys, (((1,), (1,)), ((), ())), preferred_element_type=jnp.float32
-                ) + bias[m]
-                e = jnp.exp2((s - jnp.max(s, axis=1, keepdims=True)) * factor)
-                weights = (e * (1.0 / jnp.sum(e, axis=1, keepdims=True))).astype(jnp.bfloat16)
-                obuf[m, :, at] = jnp.dot(weights, values, preferred_element_type=jnp.float32).astype(jnp.bfloat16)
-                return 0
-            lax.fori_loop(0, FAN, one, 0, unroll=True)
-        out_copy(g).start()
+        keys = kv[g, m, :, 0:HEAD]
+        values = kv[g, m, :, HEAD:WIDE]
+
+        def one(j, _):
+            at = pl.ds(pl.multiple_of((g * FAN + j) * HEAD, HEAD), HEAD)
+            s = lax.dot_general(
+                qbuf[m, :, at], keys, (((1,), (1,)), ((), ())), preferred_element_type=jnp.float32
+            ) + bias[m]
+            e = jnp.exp2((s - jnp.max(s, axis=1, keepdims=True)) * factor)
+            weights = (e * (1.0 / jnp.sum(e, axis=1, keepdims=True))).astype(jnp.bfloat16)
+            out[0, m, :, at] = jnp.dot(weights, values, preferred_element_type=jnp.float32).astype(jnp.bfloat16)
+            return 0
+        lax.fori_loop(0, FAN, one, 0, unroll=True)
 
     for g in (0, 1, 2):
         for c in w_loads[g]:
             c.wait()
-        w_start(g, 0)
+        w_step(g, 0)
         if g == 0:
             x_other.wait()
             x_copy(0).start()
     for c in w_loads[3]:
         c.wait()
-    x_mine.wait()
-    g_load.wait()
-    l_load.wait()
-    q_load.wait()
+    start_wait()
     squares()
     inv_copy().start()
     for j in range(1, XCUT):
@@ -246,72 +358,117 @@
     w_step(0, 2)
     w_step(1, 2)
     w_step(0, 3)
-    inv_copy().wait_recv()
-    x_copy(0).wait_recv()
+    inv_wait()
+    x_wait(0)
     normalise_partner(0)
     w_step(1, 3)
     w_step(0, 4)
     w_step(1, 4)
-    w_start(3, 0)
-    x_copy(1).wait_recv()
+    w_step(3, 0)
+    x_wait(1)
     normalise_partner(1)
     w_step(2, 1)
-    w_arrive(0, 4)
+    w_rest(0, ARRIVALS[0])
     dot_own(0)
+    w_rest(1, ARRIVALS[1])
+    dot_own(1)
     w_step(3, 1)
-    w_arrive(1, 4)
-    dot_own(1)
     w_step(2, 2)
-    x_copy(2).wait_recv()
+    x_wait(2)
     normalise_partner(2)
     w_step(3, 2)
     w_step(2, 3)
-    x_copy(3).wait_recv()
+    x_wait(3)
     normalise_partner(3)
+    w_step(3, 3, (0, 2, 1), (0, 3))
+    w_step(3, 3, (1,))
     dot_partner(0)
-    part_copy(0).start()
-    w_step(3, 3)
     dot_partner(1)
-    part_copy(1).start()
+    w_step(3, 3, (2,), (0, -3))
+    w_rest(2, w_early(2))
+    dot_early(2)
+    for m in range(MICRO):
+        part_wait(0, m)
+        finish_kv(0, m)
     w_step(2, 4)
-    finish_kv(0)
-    w_step(3, 4)
-    finish_kv(1)
-    w_arrive(2, 4)
-    dot_partner(2)
-    part_copy(2).start()
-    dot_own(2)
-    w_arrive(3, 4)
-    dot_partner(3)
-    part_copy(3).start()
-    dot_own(3)
-    finish_kv(2)
-    attend(0)
-    finish_kv(3)
-    attend(1)
-    attend(2)
-    attend(3)
-
-    for g in range(GROUPS):
-        for p in range(5):
-            for link in (0, 1, 2):
-                w_copy(link, g, p, block_at(*links[link][2][p])).wait_send()
-    for j in range(XCUT):
-        x_copy(j).wait_send()
-    inv_copy().wait_send()
-    for g in range(GROUPS):
-        part_copy(g).wait_send()
-        halo_copy(g).wait_send()
-        out_copy(g).wait()
+    w_step(3, 4, (2,))
+    w_rest(3, w_early(3))
+    dot_early(3)
+    w_step(3, 4, (1,))
+    for m in range(MICRO):
+        part_wait(1, m)
+        finish_kv(1, m)
+    relay(0)
+    w_rest(2, w_late(2))
+    dot_late(2)
+
+    @pl.when((z > 0) | (y == 0))
+    def _():
+        for m in range(MICRO):
+            halo_wait(0, m)
+            attend(0, m)
+
+    relay(1)
+    w_rest(3, w_late(3))
+    dot_late(3)
+
+    @pl.when((z == 0) & (y > 0))
+    def _():
+        for m in range(MICRO):
+            halo_wait(0, m)
+            attend(0, m)
+
+    for m in range(MICRO):
+        part_wait(2, m)
+        finish_kv(2, m)
+    part_wait(3, 0)
+    finish_kv(3, 0)
+    halo_wait(1, 0)
+    attend(1, 0)
+    relay(2)
+    part_wait(3, 1)
+    finish_kv(3, 1)
+    halo_wait(1, 1)
+    attend(1, 1)
+    relay(3)
+    for g in (2, 3):
+        for m in range(MICRO):
+            halo_wait(g, m)
+            attend(g, m)
+
+    def tail_wait():
+        for g in range(GROUPS):
+            for k in (0, 1, 2):
+                for i, (_, item) in enumerate(SENDS[g][k]):
+                    w_copy(g, k, i, block_at(*item)).wait_send()
+        for j in range(XCUT):
+            x_copy(j).wait_send()
+        inv_copy().wait_send()
+        for g in range(GROUPS):
+            for m in range(MICRO):
+                part_copy(g, m).wait_send()
+
+        @pl.when(me < 31)
+        def _():
+            for g in range(GROUPS):
+                for m in range(MICRO):
+                    halo_to(g, m, z_next).wait_send()
+
+        @pl.when(((z == 0) & (y < 3)) | ((z == 7) & (y > 0)))
+        def _():
+            for g in (0, 1):
+                pass_on(g, 0, z_next).wait_send()
+
+    tail_wait()
 
 
 def body(tokens, queries, gains, key_weight, value_weight, lengths):
     bf16, f32 = jnp.bfloat16, jnp.float32
     return pl.pallas_call(
         kernel,
-        out_shape=jax.ShapeDtypeStruct(queries.shape, bf16),
+        out_shape=pltpu.VMEM(queries.shape, bf16),
         in_specs=[pl.BlockSpec(memory_space=pl.ANY)] * 6,
-        out_specs=pl.BlockSpec(memory_space=pl.ANY),
+        out_specs=pl.BlockSpec(memory_space=pltpu.VMEM),
         scratch_shapes=[
             pltpu.VMEM((GROUPS, HALF, WIDE), bf16),
             pltpu.VMEM((MICRO, TOK, HALF), bf16),
@@ -320,28 +477,30 @@
             pltpu.VMEM((4 * TOK, HALF), bf16),
             pltpu.VMEM((1, HALF), bf16),
             pltpu.VMEM((MICRO, TOK, GROUPS * FAN * HEAD), bf16),
-            pltpu.VMEM((MICRO, TOK, GROUPS * FAN * HEAD), bf16),
             pltpu.VMEM((MICRO, DOCS), jnp.int32),
             pltpu.VMEM((MICRO, TOK, 128), f32),
             pltpu.VMEM((8, 128), f32),
             pltpu.VMEM((8, 128), f32),
             pltpu.VMEM((MICRO, TOK, 2 * TOK), f32),
+            pltpu.VMEM((2, 4 * TOK, WIDE), f32),
             pltpu.VMEM((GROUPS, 2 * TOK, WIDE), f32),
             pltpu.VMEM((GROUPS, 2 * TOK, WIDE), bf16),
             pltpu.VMEM((GROUPS, 2 * TOK, WIDE), bf16),
             pltpu.VMEM((GROUPS, MICRO, 2 * TOK, WIDE), bf16),
-            pltpu.SemaphoreType.DMA((3, GROUPS, 5)),
-            pltpu.SemaphoreType.DMA((3, GROUPS, 5)),
+            pltpu.VMEM((GROUPS, TOK, WIDE), bf16),
+            pltpu.SemaphoreType.DMA((3, GROUPS, 6)),
+            pltpu.SemaphoreType.DMA((3, GROUPS, 6)),
             pltpu.SemaphoreType.DMA((XCUT,)),
             pltpu.SemaphoreType.DMA((XCUT,)),
             pltpu.SemaphoreType.DMA,
             pltpu.SemaphoreType.DMA,
-            pltpu.SemaphoreType.DMA((GROUPS,)),
-            pltpu.SemaphoreType.DMA((GROUPS,)),
+            pltpu.SemaphoreType.DMA((GROUPS, MICRO)),
+            pltpu.SemaphoreType.DMA((GROUPS, MICRO)),
+            pltpu.SemaphoreType.DMA((GROUPS, MICRO)),
+            pltpu.SemaphoreType.DMA((GROUPS, MICRO)),
             pltpu.SemaphoreType.DMA((GROUPS,)),
             pltpu.SemaphoreType.DMA((GROUPS,)),
             pltpu.SemaphoreType.DMA((13,)),
-            pltpu.SemaphoreType.DMA((GROUPS,)),
         ],
         compiler_params=pltpu.CompilerParams(collective_id=0, has_side_effects=True),
         name="window",

time: 92.4 us -> 84.7 us (0.917)
  Pallas kernels: 87.9 us -> 82.8 us
  local copies, waits for them, and re-layouts: 3.13 us -> 1.32 us
    pallas_call x1, Pallas kernels: 87.9 us -> 82.8 us  [body(): pl.pallas_call(kernel, out_shape=pltpu.VMEM(queries.shape, bf16), in_spec...]
    unnamed x1, local copies, waits for them, and re-layouts: 3.13 us -> 1.32 us
where the time goes in v2:
time: 84.7 us; the launch traced here: 84.1 us
  Pallas kernels  82.8 us (98%)
  local copies, waits for them, and re-layouts  1.32 us (2%)
    pallas_call x1, Pallas kernels, body(): pl.pallas_call(kernel, out_shape=pltpu.VMEM(queries.shape, bf16), in_spec...  82.8 us

profile of v2, /device:TPU:16, one launch (start us, length us, event | category | flops | bytes accessed | tf_op | source)
XLA Modules:
  0.0 84.1 jit_solution(135761254705998045)
XLA Ops:
  0.0 82.8 %window.1 = bf16[1,2,128,4096]{3,2,1,0:T(8,128)(2,1)S(1)} custom-call(bf16[1,2,128,8192]{3,2,1,0:T(8,128)(2,1)} %tok.1, bf16[1,2,128,4096]{3,2,1,0:T(8,128)(2,1)} %queries.1, bf16[1,8192]{1,0:T(2,128)(2,1)} %gains.1, bf16[1,256,512]{2,1,0:T(8,128)(2,1)} %key_w.1, bf16[1,256,512]{2,1,0:T(8,128)(2,1)} %value_w.1, s32[2,64]{1,0:T(2,128)} %lengths.1), custom_call_target="tpu_custom_call" | custom-call | tf_op jit(solution)/shard_map/window/pallas_call | solution.py:467
  82.8 1.3 %copy.8 = bf16[1,2,128,4096]{3,2,1,0:T(8,128)(2,1)} copy(bf16[1,2,128,4096]{3,2,1,0:T(8,128)(2,1)S(1)} %window.1) | data formatting | bytes 4194304

commit v3 on v2

--- a/solution.py
+++ b/solution.py
@@ -46,6 +46,11 @@
     }
     for links in SENDS
 ]
+PLACE = {}
+for _g, _links in enumerate(SENDS):
+    for _k, _link in enumerate(_links):
+        for _i in range(len(_link)):
+            PLACE[_g, _k, _i] = len(PLACE)
 LATE = ((), (), ((1, 3), (1, 4), (2, 4)), ((1, 3), (1, 4), (2, 3), (2, 4)))
 
 
@@ -112,8 +117,8 @@
         return pltpu.make_async_remote_copy(
             src_ref=wbuf.at[g, where],
             dst_ref=wbuf.at[g, where],
-            send_sem=w_send.at[k, g, i],
-            recv_sem=w_recv.at[k, g, i],
+            send_sem=w_send,
+            recv_sem=w_recv.at[PLACE[g, k, i]],
             device_id={"fsdp": targets[k]},
             device_id_type=MESH,
         )
@@ -197,20 +202,23 @@
             def _():
                 halo_to(g, m, after).start()
 
-    def relay(g):
-        if g < 2:
-            @pl.when((z == 0) & (y < 3))
-            def _():
-                halo_to(g, 1, z_next, passing.at[g]).wait_recv()
-                pass_on(g, 1, below).start()
-
-            @pl.when((z == 7) & (y > 0))
-            def _():
-                halo_to(g, 0, z_next, passing.at[g]).wait_recv()
-                pass_on(g, 0, z_next).start()
+    def relay_first(g):
+        @pl.when((z == 0) & (y < 3))
+        def _():
+            halo_to(g, 1, z_next, passing.at[g]).wait_recv()
+            pass_on(g, 1, below).start()
+
+    def relay_last(g):
+        @pl.when((z == 7) & (y > 0))
+        def _():
+            halo_to(g, 0, z_next, passing.at[g]).wait_recv()
+            pass_on(g, 0, z_next).start()
 
     def eye(n):
         return lax.broadcasted_iota(jnp.int32, (n, n), 0) == lax.broadcasted_iota(jnp.int32, (n, n), 1)
+
+    def window():
+        return lax.broadcasted_iota(jnp.int32, (TOK, TOK), 1) <= lax.broadcasted_iota(jnp.int32, (TOK, TOK), 0)
 
     def squares():
         for m in range(MICRO):
@@ -263,7 +271,8 @@
             kp = lax.broadcasted_iota(jnp.int32, (TOK, 2 * TOK), 1) + (start - TOK)
             qp = lax.broadcasted_iota(jnp.int32, (TOK, 2 * TOK), 0) + start
             allowed = (key_doc == query_doc) & (kp <= qp) & (kp >= 0)
-            bias[m] = jnp.where(allowed, 0.0, -1e30)
+            merged = jnp.where(window(), jnp.where(allowed[:, TOK:], 1.0, 0.0), jnp.where(allowed[:, :TOK], 1.0, 0.0))
+            bias[m] = jnp.where(merged > 0.5, 0.0, -1e30)
 
     def dot_own(g):
         p_own[g] = jnp.dot(xn[0:2 * TOK, :], wbuf[g], preferred_element_type=jnp.float32)
@@ -324,18 +333,18 @@
     def attend(g, m):
         factor = HEAD ** (-0.5) * 1.4426950408889634
         keys = kv[g, m, :, 0:HEAD]
-        values = kv[g, m, :, HEAD:WIDE]
-
-        def one(j, _):
-            at = pl.ds(pl.multiple_of((g * FAN + j) * HEAD, HEAD), HEAD)
+        values = jnp.concatenate([kv[g, m, :, HEAD:WIDE], jnp.ones((2 * TOK, HEAD), jnp.bfloat16)], axis=1)
+        own = window()
+        for j in range(FAN):
+            at = pl.ds((g * FAN + j) * HEAD, HEAD)
             s = lax.dot_general(
                 qbuf[m, :, at], keys, (((1,), (1,)), ((), ())), preferred_element_type=jnp.float32
-            ) + bias[m]
+            )
+            s = jnp.where(own, s[:, TOK:], s[:, :TOK]) + bias[m]
             e = jnp.exp2((s - jnp.max(s, axis=1, keepdims=True)) * factor)
-            weights = (e * (1.0 / jnp.sum(e, axis=1, keepdims=True))).astype(jnp.bfloat16)
-            out[0, m, :, at] = jnp.dot(weights, values, preferred_element_type=jnp.float32).astype(jnp.bfloat16)
-            return 0
-        lax.fori_loop(0, FAN, one, 0, unroll=True)
+            weights = jnp.concatenate([jnp.where(own, 0.0, e), jnp.where(own, e, 0.0)], axis=1)
+            mixed = jnp.dot(weights.astype(jnp.bfloat16), values, preferred_element_type=jnp.float32)
+            out[0, m, :, at] = (mixed[:, :HEAD] * (1.0 / mixed[:, HEAD:])).astype(jnp.bfloat16)
 
     for g in (0, 1, 2):
         for c in w_loads[g]:
@@ -398,49 +407,65 @@
     for m in range(MICRO):
         part_wait(1, m)
         finish_kv(1, m)
-    relay(0)
+    relay_first(0)
+    relay_last(0)
     w_rest(2, w_late(2))
     dot_late(2)
-
-    @pl.when((z > 0) | (y == 0))
+    edge = (z == 0) & (y > 0)
+
+    @pl.when(jnp.logical_not(edge))
     def _():
         for m in range(MICRO):
             halo_wait(0, m)
             attend(0, m)
 
-    relay(1)
+    relay_first(1)
+    relay_last(1)
     w_rest(3, w_late(3))
     dot_late(3)
 
-    @pl.when((z == 0) & (y > 0))
+    @pl.when(edge)
     def _():
-        for m in range(MICRO):
-            halo_wait(0, m)
-            attend(0, m)
+        halo_wait(0, 0)
+        attend(0, 0)
 
     for m in range(MICRO):
         part_wait(2, m)
         finish_kv(2, m)
     part_wait(3, 0)
     finish_kv(3, 0)
-    halo_wait(1, 0)
-    attend(1, 0)
-    relay(2)
+
+    @pl.when(edge)
+    def _():
+        halo_wait(0, 1)
+        attend(0, 1)
+
+    @pl.when(jnp.logical_not(edge))
+    def _():
+        halo_wait(1, 0)
+        attend(1, 0)
+
     part_wait(3, 1)
     finish_kv(3, 1)
+
+    @pl.when(edge)
+    def _():
+        halo_wait(1, 0)
+        attend(1, 0)
+
     halo_wait(1, 1)
     attend(1, 1)
-    relay(3)
     for g in (2, 3):
         for m in range(MICRO):
             halo_wait(g, m)
             attend(g, m)
 
     def tail_wait():
-        for g in range(GROUPS):
-            for k in (0, 1, 2):
-                for i, (_, item) in enumerate(SENDS[g][k]):
-                    w_copy(g, k, i, block_at(*item)).wait_send()
+        sent = wbuf.at[:, pl.ds(0, HALF * len(PLACE) // (GROUPS * BLOCKS))]
+        pltpu.make_async_remote_copy(
+            src_ref=sent, dst_ref=sent, send_sem=w_send, recv_sem=w_recv.at[0],
+            device_id={"fsdp": mate}, device_id_type=MESH,
+        ).wait_send()
         for j in range(XCUT):
             x_copy(j).wait_send()
         inv_copy().wait_send()
@@ -481,15 +506,15 @@
             pltpu.VMEM((MICRO, TOK, 128), f32),
             pltpu.VMEM((8, 128), f32),
             pltpu.VMEM((8, 128), f32),
-            pltpu.VMEM((MICRO, TOK, 2 * TOK), f32),
+            pltpu.VMEM((MICRO, TOK, TOK), f32),
             pltpu.VMEM((2, 4 * TOK, WIDE), f32),
             pltpu.VMEM((GROUPS, 2 * TOK, WIDE), f32),
             pltpu.VMEM((GROUPS, 2 * TOK, WIDE), bf16),
             pltpu.VMEM((GROUPS, 2 * TOK, WIDE), bf16),
             pltpu.VMEM((GROUPS, MICRO, 2 * TOK, WIDE), bf16),
             pltpu.VMEM((GROUPS, TOK, WIDE), bf16),
-            pltpu.SemaphoreType.DMA((3, GROUPS, 6)),
-            pltpu.SemaphoreType.DMA((3, GROUPS, 6)),
+            pltpu.SemaphoreType.DMA,
+            pltpu.SemaphoreType.DMA((len(PLACE),)),
             pltpu.SemaphoreType.DMA((XCUT,)),
             pltpu.SemaphoreType.DMA((XCUT,)),
             pltpu.SemaphoreType.DMA,

time: 84.7 us -> 82.6 us (0.975)
  Pallas kernels: 82.8 us -> 81.2 us
    pallas_call x1, Pallas kernels: 82.8 us -> 81.2 us  [body(): pl.pallas_call(kernel, out_shape=pltpu.VMEM(queries.shape, bf16), in_spec...]
where the time goes in v3:
time: 82.6 us; the launch traced here: 82.5 us
  Pallas kernels  81.2 us (98%)
  local copies, waits for them, and re-layouts  1.32 us (2%)
    pallas_call x1, Pallas kernels, body(): pl.pallas_call(kernel, out_shape=pltpu.VMEM(queries.shape, bf16), in_spec...  81.2 us

profile of v3, /device:TPU:16, one launch (start us, length us, event | category | flops | bytes accessed | tf_op | source)
XLA Modules:
  0.0 82.5 jit_solution(9474717972295279752)
XLA Ops:
  0.0 81.2 %window.1 = bf16[1,2,128,4096]{3,2,1,0:T(8,128)(2,1)S(1)} custom-call(bf16[1,2,128,8192]{3,2,1,0:T(8,128)(2,1)} %tok.1, bf16[1,2,128,4096]{3,2,1,0:T(8,128)(2,1)} %queries.1, bf16[1,8192]{1,0:T(2,128)(2,1)} %gains.1, bf16[1,256,512]{2,1,0:T(8,128)(2,1)} %key_w.1, bf16[1,256,512]{2,1,0:T(8,128)(2,1)} %value_w.1, s32[2,64]{1,0:T(2,128)} %lengths.1), custom_call_target="tpu_custom_call" | custom-call | tf_op jit(solution)/shard_map/window/pallas_call | solution.py:492
  81.2 1.3 %copy.8 = bf16[1,2,128,4096]{3,2,1,0:T(8,128)(2,1)} copy(bf16[1,2,128,4096]{3,2,1,0:T(8,128)(2,1)S(1)} %window.1) | data formatting | bytes 4194304

commit v4 on v3

--- a/solution.py
+++ b/solution.py
@@ -31,27 +31,29 @@
     (((0, 0),), ((0, 1),), ((0, 2),), ((0, -3),), ((0, -4),)),
 )
 SIDE = (
-    (((0, 0),), ((0, 1),), ((0, 2),), ((0, 3),), ()),
-    (((0, 0),), ((0, -1),), ((0, -2),), ((1, 0),), ((1, -1),)),
-    (((0, 0),), ((0, 1),), ((0, 2),), ((0, 3), (0, -3)), ((0, 4),)),
+    (((0, 0),), ((0, 1),), ((0, 2),), ((0, 3),), ((1, 3, 1), (1, -3, 1))),
+    (((0, 0),), ((0, -1),), ((0, -2),), ((1, 0),), ((1, -1, 0),)),
+    (((0, 0),), ((0, 1),), ((0, 2),), ((0, 3), (0, -3)), ((0, 4, 0),)),
 )
 PATTERN = (EVEN, EVEN, BACK, SIDE)
 MOVES = ((0, 1), (0, -1), (1, 0))
 SENDS = [[[(p, item) for p, items in enumerate(link) for item in items] for link in pattern] for pattern in PATTERN]
 ARRIVALS = [
     {
-        ((r + MOVES[k][0]) % 2, d + MOVES[k][1]): (k, i)
+        ((r + MOVES[k][0]) % 2, d + MOVES[k][1], *part): (k, i)
         for k, link in enumerate(links)
-        for i, (_, (r, d)) in enumerate(link)
+        for i, (_, (r, d, *part)) in enumerate(link)
     }
     for links in SENDS
 ]
-PLACE = {}
+JOINT = {(g, p) for g in range(GROUPS) for p in range(5 if g < 2 else 2)}
+PLACE, _semaphores = {}, {}
 for _g, _links in enumerate(SENDS):
     for _k, _link in enumerate(_links):
-        for _i in range(len(_link)):
-            PLACE[_g, _k, _i] = len(PLACE)
-LATE = ((), (), ((1, 3), (1, 4), (2, 4)), ((1, 3), (1, 4), (2, 3), (2, 4)))
+        for _i, (_p, _) in enumerate(_link):
+            _name = (_g, _p) if (_g, _p) in JOINT else (_g, _k, _i)
+            PLACE[_g, _k, _i] = _semaphores.setdefault(_name, len(_semaphores))
+LATE = ((), (), ((0, -4), (1, -2), (1, -4)), ((1, -1), (1, -3), (1, -2), (1, 4)))
 
 
 def kernel(
@@ -83,17 +85,17 @@
     for g in range(GROUPS):
         cols = pl.ds(g * HEAD, HEAD)
         w_loads.append((
-            pltpu.make_async_copy(key_w.at[0, :, cols], wbuf.at[g, own_rows, pl.ds(0, HEAD)], local.at[2 * g]),
-            pltpu.make_async_copy(value_w.at[0, :, cols], wbuf.at[g, own_rows, pl.ds(HEAD, HEAD)], local.at[2 * g + 1]),
+            pltpu.make_async_copy(key_w.at[0, :, cols], wbuf.at[g, own_rows, pl.ds(0, HEAD)], local.at[g]),
+            pltpu.make_async_copy(value_w.at[0, :, cols], wbuf.at[g, own_rows, pl.ds(HEAD, HEAD)], local.at[g]),
         ))
     for pair in w_loads:
         for c in pair:
             c.start()
-    x_other = pltpu.make_async_copy(tok.at[0, :, :, pl.ds(other_cols, HALF)], xoth, local.at[8])
-    x_mine = pltpu.make_async_copy(tok.at[0, :, :, pl.ds(own_cols, HALF)], xown, local.at[9])
-    g_load = pltpu.make_async_copy(gains.at[:, pl.ds(own_cols, HALF)], gown, local.at[10])
-    l_load = pltpu.make_async_copy(lengths, lens, local.at[11])
-    q_load = pltpu.make_async_copy(queries.at[0], qbuf, local.at[12])
+    x_other = pltpu.make_async_copy(tok.at[0, :, :, pl.ds(other_cols, HALF)], xoth, local.at[4])
+    x_mine = pltpu.make_async_copy(tok.at[0, :, :, pl.ds(own_cols, HALF)], xown, local.at[5])
+    g_load = pltpu.make_async_copy(gains.at[:, pl.ds(own_cols, HALF)], gown, local.at[6])
+    l_load = pltpu.make_async_copy(lengths, lens, local.at[7])
+    q_load = pltpu.make_async_copy(queries.at[0], qbuf, local.at[8])
     for c in (x_other, x_mine, g_load, l_load, q_load):
         c.start()
 
@@ -113,10 +115,14 @@
     targets = (z_next, z_prev, mate)
     here = [{(0, 0)} for _ in range(GROUPS)]
 
-    def w_copy(g, k, i, where):
+    def w_ref(g, r, d, *part):
+        rows = block_at(r, d)
+        return wbuf.at[g, rows, pl.ds(part[0] * HEAD, HEAD)] if part else wbuf.at[g, rows]
+
+    def w_copy(g, k, i, ref):
         return pltpu.make_async_remote_copy(
-            src_ref=wbuf.at[g, where],
-            dst_ref=wbuf.at[g, where],
+            src_ref=ref,
+            dst_ref=ref,
             send_sem=w_send,
             recv_sem=w_recv.at[PLACE[g, k, i]],
             device_id={"fsdp": targets[k]},
@@ -124,35 +130,49 @@
         )
 
     def w_need(g, item):
-        if item not in here[g]:
-            here[g].add(item)
-            w_copy(g, *ARRIVALS[g][item], block_at(*item)).wait_recv()
+        if item in here[g]:
+            return
+        here[g].add(item)
+        if item not in ARRIVALS[g]:
+            for half in (0, 1):
+                w_need(g, (*item, half))
+            return
+        k, i = ARRIVALS[g][item]
+        p = SENDS[g][k][i][0]
+        if (g, p) in JOINT:
+            together = {it for it, (kk, ii) in ARRIVALS[g].items() if SENDS[g][kk][ii][0] == p}
+            here[g].update(together)
+            w_copy(g, k, i, wbuf.at[g, pl.ds(0, len(together) * ROWS)]).wait_recv()
+        else:
+            w_copy(g, k, i, w_ref(g, *item)).wait_recv()
 
     def w_step(g, p, links=(0, 1, 2), at=None):
         for k in links:
             for i, (position, item) in enumerate(SENDS[g][k]):
                 if position == p and at in (None, item):
-                    w_need(g, item)
-                    w_copy(g, k, i, block_at(*item)).start()
+                    w_need(g, item[:2])
+                    w_copy(g, k, i, w_ref(g, *item)).start()
 
     def w_late(g):
-        return [item for item, (k, i) in ARRIVALS[g].items() if (k, SENDS[g][k][i][0]) in LATE[g] and not (
-            g == 3 and k == 2 and SENDS[g][k][i][1] == (0, 3))]
+        return LATE[g]
 
     def w_early(g):
-        late = w_late(g)
-        return [(0, 0)] + [item for item in ARRIVALS[g] if item not in late]
+        return [(0, 0)] + [item for item in ARRIVALS[g] if item[:2] not in LATE[g]]
 
     def w_rest(g, items):
         for item in items:
             w_need(g, item)
+
+    def w_loaded(g):
+        both = wbuf.at[g, own_rows]
+        pltpu.make_async_copy(both, both, local.at[g]).wait()
 
     def x_copy(j):
         width = HALF // XCUT
         return pltpu.make_async_remote_copy(
             src_ref=xoth.at[:, :, pl.ds(j * width, width)],
             dst_ref=xprt.at[:, :, pl.ds(j * width, width)],
-            send_sem=x_send.at[j],
+            send_sem=x_send,
             recv_sem=x_recv.at[j],
             device_id={"fsdp": partner},
             device_id_type=MESH,
@@ -164,43 +184,56 @@
             device_id={"fsdp": partner}, device_id_type=MESH,
         )
 
-    def part_copy(g, m):
-        at = pl.ds(m * TOK, TOK)
+    def pieces(g):
+        return ((0, WIDE),) if g < 3 else ((0, HEAD), (HEAD, HEAD))
+
+    def part_copy(g, m, c):
+        first, width = pieces(g)[c]
+        at = (g, pl.ds(m * TOK, TOK), pl.ds(first, width))
         return pltpu.make_async_remote_copy(
-            src_ref=p_send.at[g, at], dst_ref=p_recv.at[g, at],
-            send_sem=p_ssem.at[g, m], recv_sem=p_rsem.at[g, m],
+            src_ref=p_send.at[at], dst_ref=p_recv.at[at],
+            send_sem=p_ssem, recv_sem=p_rsem.at[g + c, m],
             device_id={"fsdp": partner}, device_id_type=MESH,
         )
 
-    def halo_to(g, m, device, into=None):
+    def halo_to(g, m, device, into=None, c=0):
+        first, width = pieces(g)[c]
         return pltpu.make_async_remote_copy(
-            src_ref=kv.at[g, m, pl.ds(TOK, TOK)],
-            dst_ref=kv.at[g, m, pl.ds(0, TOK)] if into is None else into,
-            send_sem=h_send.at[g, m],
-            recv_sem=(h_recv.at[g, m] if into is None else r_recv.at[g]),
+            src_ref=kv.at[g, m, pl.ds(TOK, TOK), pl.ds(first, width)],
+            dst_ref=kv.at[g, m, pl.ds(0, TOK), pl.ds(first, width)] if into is None else into,
+            send_sem=h_send,
+            recv_sem=(h_recv.at[g + c, m] if into is None else r_recv.at[g]),
             device_id={"fsdp": device}, device_id_type=MESH,
         )
 
     def pass_on(g, m, device):
         return pltpu.make_async_remote_copy(
             src_ref=passing.at[g], dst_ref=kv.at[g, m, pl.ds(0, TOK)],
-            send_sem=r_send.at[g], recv_sem=h_recv.at[g, m],
+            send_sem=r_send, recv_sem=h_recv.at[g, m],
             device_id={"fsdp": device}, device_id_type=MESH,
         )
 
-    def halo_start(g, m):
+    def halo_start(g, m, c):
         @pl.when(z < 7)
         def _():
-            halo_to(g, m, z_next).start()
+            halo_to(g, m, z_next, c=c).start()
 
         if g < 2:
             @pl.when((z == 7) & (y < 3))
             def _():
                 halo_to(g, m, z_next if m == 1 else below, passing.at[g]).start()
         else:
-            @pl.when((z == 7) & (y < 3))
+            @pl.when((z == 7) & ((y == 0) | (y == 2)))
             def _():
-                halo_to(g, m, after).start()
+                halo_to(g, m, after, c=c).start()
+
+    def halo_last():
+        @pl.when((z == 7) & (y == 1))
+        def _():
+            for g in (2, 3):
+                for m in range(MICRO):
+                    for c in range(len(pieces(g))):
+                        halo_to(g, m, after, c=c).start()
 
     def relay_first(g):
         @pl.when((z == 0) & (y < 3))
@@ -282,7 +315,7 @@
             xn[2 * TOK:4 * TOK, :], wbuf[g], preferred_element_type=jnp.float32
         ).astype(jnp.bfloat16)
         for m in range(MICRO):
-            part_copy(g, m).start()
+            part_copy(g, m, 0).start()
 
     def add_blocks(total, g, items, first, count):
         for item in items:
@@ -304,16 +337,18 @@
             p_send[g, m * TOK:(m + 1) * TOK] = add_blocks(
                 acc[g - 2, first:first + TOK], g, w_late(g), first, TOK
             ).astype(jnp.bfloat16)
-            part_copy(g, m).start()
+            for c in range(len(pieces(g))):
+                part_copy(g, m, c).start()
         p_own[g] = add_blocks(acc[g - 2, 0:2 * TOK], g, w_late(g), 0, 2 * TOK)
 
-    def part_wait(g, m):
-        part_copy(g, m).wait_recv()
+    def part_wait(g, m, c=0):
+        part_copy(g, m, c).wait_recv()
 
     def halo_wait(g, m):
         @pl.when(me > 0)
         def _():
-            halo_to(g, m, z_next).wait_recv()
+            for c in range(len(pieces(g))):
+                halo_to(g, m, z_next, c=c).wait_recv()
 
     def x_wait(j):
         x_copy(j).wait_recv()
@@ -327,8 +362,12 @@
 
     def finish_kv(g, m):
         at = pl.ds(m * TOK, TOK)
-        kv[g, m, TOK:2 * TOK, :] = (p_own[g, at] + p_recv[g, at].astype(jnp.float32)).astype(jnp.bfloat16)
-        halo_start(g, m)
+        for c, (first, width) in enumerate(pieces(g)):
+            if c > 0:
+                part_wait(g, m, c)
+            cols = pl.ds(first, width)
+            kv[g, m, TOK:2 * TOK, cols] = (p_own[g, at, cols] + p_recv[g, at, cols].astype(jnp.float32)).astype(jnp.bfloat16)
+            halo_start(g, m, c)
 
     def attend(g, m):
         factor = HEAD ** (-0.5) * 1.4426950408889634
@@ -347,14 +386,12 @@
             out[0, m, :, at] = (mixed[:, :HEAD] * (1.0 / mixed[:, HEAD:])).astype(jnp.bfloat16)
 
     for g in (0, 1, 2):
-        for c in w_loads[g]:
-            c.wait()
+        w_loaded(g)
         w_step(g, 0)
         if g == 0:
             x_other.wait()
             x_copy(0).start()
-    for c in w_loads[3]:
-        c.wait()
+    w_loaded(3)
     start_wait()
     squares()
     inv_copy().start()
@@ -401,9 +438,11 @@
         finish_kv(0, m)
     w_step(2, 4)
     w_step(3, 4, (2,))
+    w_step(3, 4, (0,), (1, 3, 1))
     w_rest(3, w_early(3))
     dot_early(3)
     w_step(3, 4, (1,))
+    w_step(3, 4, (0,), (1, -3, 1))
     for m in range(MICRO):
         part_wait(1, m)
         finish_kv(1, m)
@@ -419,10 +458,10 @@
             halo_wait(0, m)
             attend(0, m)
 
+    w_rest(3, w_late(3))
+    dot_late(3)
     relay_first(1)
     relay_last(1)
-    w_rest(3, w_late(3))
-    dot_late(3)
 
     @pl.when(edge)
     def _():
@@ -447,42 +486,50 @@
 
     part_wait(3, 1)
     finish_kv(3, 1)
+    halo_last()
+    halo_wait(1, 1)
+    attend(1, 1)
 
     @pl.when(edge)
     def _():
         halo_wait(1, 0)
         attend(1, 0)
 
-    halo_wait(1, 1)
-    attend(1, 1)
     for g in (2, 3):
         for m in range(MICRO):
             halo_wait(g, m)
             attend(g, m)
 
     def tail_wait():
-        sent = wbuf.at[:, pl.ds(0, HALF * len(PLACE) // (GROUPS * BLOCKS))]
+        sent = wbuf.at[:, pl.ds(0, HALF - ROWS)]
         pltpu.make_async_remote_copy(
             src_ref=sent, dst_ref=sent, send_sem=w_send, recv_sem=w_recv.at[0],
             device_id={"fsdp": mate}, device_id_type=MESH,
         ).wait_send()
-        for j in range(XCUT):
-            x_copy(j).wait_send()
+        pltpu.make_async_remote_copy(
+            src_ref=xoth, dst_ref=xprt, send_sem=x_send, recv_sem=x_recv.at[0],
+            device_id={"fsdp": partner}, device_id_type=MESH,
+        ).wait_send()
         inv_copy().wait_send()
-        for g in range(GROUPS):
-            for m in range(MICRO):
-                part_copy(g, m).wait_send()
+        pltpu.make_async_remote_copy(
+            src_ref=p_send, dst_ref=p_recv, send_sem=p_ssem, recv_sem=p_rsem.at[0, 0],
+            device_id={"fsdp": partner}, device_id_type=MESH,
+        ).wait_send()
 
         @pl.when(me < 31)
         def _():
-            for g in range(GROUPS):
-                for m in range(MICRO):
-                    halo_to(g, m, z_next).wait_send()
+            rows = kv.at[:, :, pl.ds(0, TOK)]
+            pltpu.make_async_remote_copy(
+                src_ref=rows, dst_ref=rows, send_sem=h_send, recv_sem=h_recv.at[0, 0],
+                device_id={"fsdp": z_next}, device_id_type=MESH,
+            ).wait_send()
 
         @pl.when(((z == 0) & (y < 3)) | ((z == 7) & (y > 0)))
         def _():
-            for g in (0, 1):
-                pass_on(g, 0, z_next).wait_send()
+            pltpu.make_async_remote_copy(
+                src_ref=passing, dst_ref=passing, send_sem=r_send, recv_sem=r_recv.at[0],
+                device_id={"fsdp": z_next}, device_id_type=MESH,
+            ).wait_send()
 
     tail_wait()
 
@@ -512,20 +559,20 @@
             pltpu.VMEM((GROUPS, 2 * TOK, WIDE), bf16),
             pltpu.VMEM((GROUPS, 2 * TOK, WIDE), bf16),
             pltpu.VMEM((GROUPS, MICRO, 2 * TOK, WIDE), bf16),
-            pltpu.VMEM((GROUPS, TOK, WIDE), bf16),
-            pltpu.SemaphoreType.DMA,
-            pltpu.SemaphoreType.DMA((len(PLACE),)),
+            pltpu.VMEM((2, TOK, WIDE), bf16),
+            pltpu.SemaphoreType.DMA,
+            pltpu.SemaphoreType.DMA((len(_semaphores),)),
+            pltpu.SemaphoreType.DMA,
             pltpu.SemaphoreType.DMA((XCUT,)),
-            pltpu.SemaphoreType.DMA((XCUT,)),
-            pltpu.SemaphoreType.DMA,
-            pltpu.SemaphoreType.DMA,
-            pltpu.SemaphoreType.DMA((GROUPS, MICRO)),
-            pltpu.SemaphoreType.DMA((GROUPS, MICRO)),
-            pltpu.SemaphoreType.DMA((GROUPS, MICRO)),
-            pltpu.SemaphoreType.DMA((GROUPS, MICRO)),
-            pltpu.SemaphoreType.DMA((GROUPS,)),
-            pltpu.SemaphoreType.DMA((GROUPS,)),
-            pltpu.SemaphoreType.DMA((13,)),
+            pltpu.SemaphoreType.DMA,
+            pltpu.SemaphoreType.DMA,
+            pltpu.SemaphoreType.DMA,
+            pltpu.SemaphoreType.DMA((GROUPS + 1, MICRO)),
+            pltpu.SemaphoreType.DMA,
+            pltpu.SemaphoreType.DMA((GROUPS + 1, MICRO)),
+            pltpu.SemaphoreType.DMA,
+            pltpu.SemaphoreType.DMA((2,)),
+            pltpu.SemaphoreType.DMA((9,)),
         ],
         compiler_params=pltpu.CompilerParams(collective_id=0, has_side_effects=True),
         name="window",

time: 82.6 us -> 81.9 us (level)
  no operation moved by 1% of the time
where the time goes in v4:
time: 81.9 us
  Pallas kernels  80.5 us (98%)
  local copies, waits for them, and re-layouts  1.32 us (2%)
    pallas_call x1, Pallas kernels, body(): pl.pallas_call(kernel, out_shape=pltpu.VMEM(queries.shape, bf16), in_spec...  80.5 us

profile of v4, /device:TPU:16, one launch (start us, length us, event | category | flops | bytes accessed | tf_op | source)
XLA Modules:
  0.0 81.9 jit_solution(17286867602187738162)
XLA Ops:
  0.0 80.5 %window.1 = bf16[1,2,128,4096]{3,2,1,0:T(8,128)(2,1)S(1)} custom-call(bf16[1,2,128,8192]{3,2,1,0:T(8,128)(2,1)} %tok.1, bf16[1,2,128,4096]{3,2,1,0:T(8,128)(2,1)} %queries.1, bf16[1,8192]{1,0:T(2,128)(2,1)} %gains.1, bf16[1,256,512]{2,1,0:T(8,128)(2,1)} %key_w.1, bf16[1,256,512]{2,1,0:T(8,128)(2,1)} %value_w.1, s32[2,64]{1,0:T(2,128)} %lengths.1), custom_call_target="tpu_custom_call" | custom-call | tf_op jit(solution)/shard_map/window/pallas_call | solution.py:539
  80.6 1.3 %copy.8 = bf16[1,2,128,4096]{3,2,1,0:T(8,128)(2,1)} copy(bf16[1,2,128,4096]{3,2,1,0:T(8,128)(2,1)S(1)} %window.1) | data formatting | bytes 4194304

commit v5 on v4

--- a/solution.py
+++ b/solution.py
@@ -60,11 +60,12 @@
     tok, queries, gains, key_w, value_w, lengths, out,
     wbuf, xown, xoth, xprt, xn, gown, qbuf, lens, inv_own, inv_send, inv_recv,
     bias, acc, p_own, p_send, p_recv, kv, passing,
-    w_send, w_recv, x_send, x_recv, i_send, i_recv, p_ssem, p_rsem, h_send, h_recv, r_send, r_recv, local,
+    w_send, w_recv, x_send, x_recv, i_send, i_recv, p_ssem, p_rsem, h_send, h_recv, r_send, r_recv, b_send, local,
 ):
     me = lax.axis_index("fsdp")
     y, z = me // 8, me % 8
     half, row = y // 2, y % 2
+    second = lax.axis_index("section") % 2 == 1
     z_next, z_prev = y * 8 + (z + 1) % 8, y * 8 + (z + 7) % 8
     mate = (y + 1 - 2 * row) * 8 + z
     partner = (3 - y) * 8 + z
@@ -196,13 +197,13 @@
             device_id={"fsdp": partner}, device_id_type=MESH,
         )
 
-    def halo_to(g, m, device, into=None, c=0):
+    def halo_to(g, m, device, into=None, slot=0, c=0):
         first, width = pieces(g)[c]
         return pltpu.make_async_remote_copy(
             src_ref=kv.at[g, m, pl.ds(TOK, TOK), pl.ds(first, width)],
             dst_ref=kv.at[g, m, pl.ds(0, TOK), pl.ds(first, width)] if into is None else into,
             send_sem=h_send,
-            recv_sem=(h_recv.at[g + c, m] if into is None else r_recv.at[g]),
+            recv_sem=(h_recv.at[g + c, m] if into is None else r_recv.at[g + slot]),
             device_id={"fsdp": device}, device_id_type=MESH,
         )
 
@@ -227,13 +228,33 @@
             def _():
                 halo_to(g, m, after, c=c).start()
 
+            if g == 2:
+                @pl.when((z == 7) & (y == 1) & second)
+                def _():
+                    halo_to(g, m, below, passing.at[2 + m], m).start()
+
     def halo_last():
-        @pl.when((z == 7) & (y == 1))
-        def _():
-            for g in (2, 3):
-                for m in range(MICRO):
-                    for c in range(len(pieces(g))):
-                        halo_to(g, m, after, c=c).start()
+        for groups, turn in (((2, 3), jnp.logical_not(second)), ((3,), second)):
+            @pl.when((z == 7) & (y == 1) & turn)
+            def _():
+                for g in groups:
+                    for m in range(MICRO):
+                        for c in range(len(pieces(g))):
+                            halo_to(g, m, after, c=c).start()
+
+    def pass_round(m):
+        return pltpu.make_async_remote_copy(
+            src_ref=passing.at[2 + m], dst_ref=kv.at[2, m, pl.ds(0, TOK)],
+            send_sem=b_send, recv_sem=h_recv.at[2, m],
+            device_id={"fsdp": z_next}, device_id_type=MESH,
+        )
+
+    def relay_round():
+        @pl.when((z == 7) & (y == 2) & second)
+        def _():
+            for m in range(MICRO):
+                halo_to(2, m, z_next, passing.at[2 + m], m).wait_recv()
+                pass_round(m).start()
 
     def relay_first(g):
         @pl.when((z == 0) & (y < 3))
@@ -452,7 +473,7 @@
     dot_late(2)
     edge = (z == 0) & (y > 0)
 
-    @pl.when(jnp.logical_not(edge))
+    @pl.when(jnp.logical_not(edge) & (z < 7))
     def _():
         for m in range(MICRO):
             halo_wait(0, m)
@@ -486,9 +507,17 @@
 
     part_wait(3, 1)
     finish_kv(3, 1)
+    @pl.when(z == 7)
+    def _():
+        for m in range(MICRO):
+            halo_wait(0, m)
+            attend(0, m)
+
     halo_last()
+
     halo_wait(1, 1)
     attend(1, 1)
+    relay_round()
 
     @pl.when(edge)
     def _():
@@ -527,7 +556,15 @@
         @pl.when(((z == 0) & (y < 3)) | ((z == 7) & (y > 0)))
         def _():
             pltpu.make_async_remote_copy(
-                src_ref=passing, dst_ref=passing, send_sem=r_send, recv_sem=r_recv.at[0],
+                src_ref=passing.at[pl.ds(0, 2)], dst_ref=passing.at[pl.ds(0, 2)], send_sem=r_send, recv_sem=r_recv.at[0],
+                device_id={"fsdp": z_next}, device_id_type=MESH,
+            ).wait_send()
+
+        @pl.when((z == 7) & (y == 2) & second)
+        def _():
+            both = passing.at[pl.ds(2, 2)]
+            pltpu.make_async_remote_copy(
+                src_ref=both, dst_ref=both, send_sem=b_send, recv_sem=r_recv.at[2],
                 device_id={"fsdp": z_next}, device_id_type=MESH,
             ).wait_send()
 
@@ -559,7 +596,7 @@
             pltpu.VMEM((GROUPS, 2 * TOK, WIDE), bf16),
             pltpu.VMEM((GROUPS, 2 * TOK, WIDE), bf16),
             pltpu.VMEM((GROUPS, MICRO, 2 * TOK, WIDE), bf16),
-            pltpu.VMEM((2, TOK, WIDE), bf16),
+            pltpu.VMEM((4, TOK, WIDE), bf16),
             pltpu.SemaphoreType.DMA,
             pltpu.SemaphoreType.DMA((len(_semaphores),)),
             pltpu.SemaphoreType.DMA,
@@ -571,7 +608,8 @@
             pltpu.SemaphoreType.DMA,
             pltpu.SemaphoreType.DMA((GROUPS + 1, MICRO)),
             pltpu.SemaphoreType.DMA,
-            pltpu.SemaphoreType.DMA((2,)),
+            pltpu.SemaphoreType.DMA((4,)),
+            pltpu.SemaphoreType.DMA,
             pltpu.SemaphoreType.DMA((9,)),
         ],
         compiler_params=pltpu.CompilerParams(collective_id=0, has_side_effects=True),

time: 81.9 us -> 81.6 us (level)
  no operation moved by 1% of the time
where the time goes in v5:
time: 81.6 us; the launch traced here: 81.4 us
  Pallas kernels  80.1 us (98%)
  local copies, waits for them, and re-layouts  1.32 us (2%)
    pallas_call x1, Pallas kernels, body(): pl.pallas_call(kernel, out_shape=pltpu.VMEM(queries.shape, bf16), in_spec...  80.1 us

profile of v5, /device:TPU:16, one launch (start us, length us, event | category | flops | bytes accessed | tf_op | source)
XLA Modules:
  0.0 81.4 jit_solution(6440555351858067704)
XLA Ops:
  0.0 80.1 %window.1 = bf16[1,2,128,4096]{3,2,1,0:T(8,128)(2,1)S(1)} custom-call(bf16[1,2,128,8192]{3,2,1,0:T(8,128)(2,1)} %tok.1, bf16[1,2,128,4096]{3,2,1,0:T(8,128)(2,1)} %queries.1, bf16[1,8192]{1,0:T(2,128)(2,1)} %gains.1, bf16[1,256,512]{2,1,0:T(8,128)(2,1)} %key_w.1, bf16[1,256,512]{2,1,0:T(8,128)(2,1)} %value_w.1, s32[2,64]{1,0:T(2,128)} %lengths.1), custom_call_target="tpu_custom_call" | custom-call | tf_op jit(solution)/shard_map/window/pallas_call | solution.py:576
  80.1 1.3 %copy.8 = bf16[1,2,128,4096]{3,2,1,0:T(8,128)(2,1)} copy(bf16[1,2,128,4096]{3,2,1,0:T(8,128)(2,1)S(1)} %window.1) | data formatting | bytes 4194304

commit v6 on v5

--- a/solution.py
+++ b/solution.py
@@ -365,11 +365,10 @@
     def part_wait(g, m, c=0):
         part_copy(g, m, c).wait_recv()
 
-    def halo_wait(g, m):
+    def halo_wait(g, m, c=0):
         @pl.when(me > 0)
         def _():
-            for c in range(len(pieces(g))):
-                halo_to(g, m, z_next, c=c).wait_recv()
+            halo_to(g, m, z_next, c=c).wait_recv()
 
     def x_wait(j):
         x_copy(j).wait_recv()
@@ -393,8 +392,8 @@
     def attend(g, m):
         factor = HEAD ** (-0.5) * 1.4426950408889634
         keys = kv[g, m, :, 0:HEAD]
-        values = jnp.concatenate([kv[g, m, :, HEAD:WIDE], jnp.ones((2 * TOK, HEAD), jnp.bfloat16)], axis=1)
         own = window()
+        held = []
         for j in range(FAN):
             at = pl.ds((g * FAN + j) * HEAD, HEAD)
             s = lax.dot_general(
@@ -403,7 +402,13 @@
             s = jnp.where(own, s[:, TOK:], s[:, :TOK]) + bias[m]
             e = jnp.exp2((s - jnp.max(s, axis=1, keepdims=True)) * factor)
             weights = jnp.concatenate([jnp.where(own, 0.0, e), jnp.where(own, e, 0.0)], axis=1)
-            mixed = jnp.dot(weights.astype(jnp.bfloat16), values, preferred_element_type=jnp.float32)
+            held.append(weights.astype(jnp.bfloat16))
+        if len(pieces(g)) > 1:
+            halo_wait(g, m, 1)
+        values = jnp.concatenate([kv[g, m, :, HEAD:WIDE], jnp.ones((2 * TOK, HEAD), jnp.bfloat16)], axis=1)
+        for j in range(FAN):
+            at = pl.ds((g * FAN + j) * HEAD, HEAD)
+            mixed = jnp.dot(held[j], values, preferred_element_type=jnp.float32)
             out[0, m, :, at] = (mixed[:, :HEAD] * (1.0 / mixed[:, HEAD:])).astype(jnp.bfloat16)
 
     for g in (0, 1, 2):

time: 81.6 us -> 81.5 us (level)
  no operation moved by 1% of the time
where the time goes in v6:
time: 81.5 us; the launch traced here: 81.2 us
  Pallas kernels  79.9 us (98%)
  local copies, waits for them, and re-layouts  1.32 us (2%)
    pallas_call x1, Pallas kernels, body(): pl.pallas_call(kernel, out_shape=pltpu.VMEM(queries.shape, bf16), in_spec...  79.9 us

profile of v6, /device:TPU:16, one launch (start us, length us, event | category | flops | bytes accessed | tf_op | source)
XLA Modules:
  0.0 81.2 jit_solution(7540617664613428349)
XLA Ops:
  0.0 79.9 %window.1 = bf16[1,2,128,4096]{3,2,1,0:T(8,128)(2,1)S(1)} custom-call(bf16[1,2,128,8192]{3,2,1,0:T(8,128)(2,1)} %tok.1, bf16[1,2,128,4096]{3,2,1,0:T(8,128)(2,1)} %queries.1, bf16[1,8192]{1,0:T(2,128)(2,1)} %gains.1, bf16[1,256,512]{2,1,0:T(8,128)(2,1)} %key_w.1, bf16[1,256,512]{2,1,0:T(8,128)(2,1)} %value_w.1, s32[2,64]{1,0:T(2,128)} %lengths.1), custom_call_target="tpu_custom_call" | custom-call | tf_op jit(solution)/shard_map/window/pallas_call | solution.py:581
  79.9 1.3 %copy.8 = bf16[1,2,128,4096]{3,2,1,0:T(8,128)(2,1)} copy(bf16[1,2,128,4096]{3,2,1,0:T(8,128)(2,1)S(1)} %window.1) | data formatting | bytes 4194304

commit v7 on v6

--- a/solution.py
+++ b/solution.py
@@ -197,13 +197,13 @@
             device_id={"fsdp": partner}, device_id_type=MESH,
         )
 
-    def halo_to(g, m, device, into=None, slot=0, c=0):
+    def halo_to(g, m, device, into=None, c=0):
         first, width = pieces(g)[c]
         return pltpu.make_async_remote_copy(
             src_ref=kv.at[g, m, pl.ds(TOK, TOK), pl.ds(first, width)],
             dst_ref=kv.at[g, m, pl.ds(0, TOK), pl.ds(first, width)] if into is None else into,
             send_sem=h_send,
-            recv_sem=(h_recv.at[g + c, m] if into is None else r_recv.at[g + slot]),
+            recv_sem=(h_recv.at[g + c, m] if into is None else r_recv.at[g]),
             device_id={"fsdp": device}, device_id_type=MESH,
         )
 
@@ -228,33 +228,31 @@
             def _():
                 halo_to(g, m, after, c=c).start()
 
-            if g == 2:
+            if (g, m) == (2, 0):
                 @pl.when((z == 7) & (y == 1) & second)
                 def _():
-                    halo_to(g, m, below, passing.at[2 + m], m).start()
+                    halo_to(g, m, below, passing.at[2]).start()
 
     def halo_last():
-        for groups, turn in (((2, 3), jnp.logical_not(second)), ((3,), second)):
+        for first, turn in ((0, jnp.logical_not(second)), (1, second)):
             @pl.when((z == 7) & (y == 1) & turn)
             def _():
-                for g in groups:
-                    for m in range(MICRO):
-                        for c in range(len(pieces(g))):
-                            halo_to(g, m, after, c=c).start()
-
-    def pass_round(m):
+                for g, m in ((2, 0), (2, 1), (3, 0), (3, 1))[first:]:
+                    for c in range(len(pieces(g))):
+                        halo_to(g, m, after, c=c).start()
+
+    def pass_round():
         return pltpu.make_async_remote_copy(
-            src_ref=passing.at[2 + m], dst_ref=kv.at[2, m, pl.ds(0, TOK)],
-            send_sem=b_send, recv_sem=h_recv.at[2, m],
+            src_ref=passing.at[2], dst_ref=kv.at[2, 0, pl.ds(0, TOK)],
+            send_sem=b_send, recv_sem=h_recv.at[2, 0],
             device_id={"fsdp": z_next}, device_id_type=MESH,
         )
 
     def relay_round():
         @pl.when((z == 7) & (y == 2) & second)
         def _():
-            for m in range(MICRO):
-                halo_to(2, m, z_next, passing.at[2 + m], m).wait_recv()
-                pass_round(m).start()
+            halo_to(2, 0, z_next, passing.at[2]).wait_recv()
+            pass_round().start()
 
     def relay_first(g):
         @pl.when((z == 0) & (y < 3))
@@ -514,11 +512,16 @@
     finish_kv(3, 1)
     @pl.when(z == 7)
     def _():
-        for m in range(MICRO):
-            halo_wait(0, m)
-            attend(0, m)
+        halo_wait(0, 0)
+        attend(0, 0)
 
     halo_last()
+
+    @pl.when(z == 7)
+    def _():
+        halo_wait(0, 1)
+        attend(0, 1)
+
 
     halo_wait(1, 1)
     attend(1, 1)
@@ -567,11 +570,7 @@
 
         @pl.when((z == 7) & (y == 2) & second)
         def _():
-            both = passing.at[pl.ds(2, 2)]
-            pltpu.make_async_remote_copy(
-                src_ref=both, dst_ref=both, send_sem=b_send, recv_sem=r_recv.at[2],
-                device_id={"fsdp": z_next}, device_id_type=MESH,
-            ).wait_send()
+            pass_round().wait_send()
 
     tail_wait()
 
@@ -601,7 +600,7 @@
             pltpu.VMEM((GROUPS, 2 * TOK, WIDE), bf16),
             pltpu.VMEM((GROUPS, 2 * TOK, WIDE), bf16),
             pltpu.VMEM((GROUPS, MICRO, 2 * TOK, WIDE), bf16),
-            pltpu.VMEM((4, TOK, WIDE), bf16),
+            pltpu.VMEM((3, TOK, WIDE), bf16),
             pltpu.SemaphoreType.DMA,
             pltpu.SemaphoreType.DMA((len(_semaphores),)),
             pltpu.SemaphoreType.DMA,
@@ -613,7 +612,7 @@
             pltpu.SemaphoreType.DMA,
             pltpu.SemaphoreType.DMA((GROUPS + 1, MICRO)),
             pltpu.SemaphoreType.DMA,
-            pltpu.SemaphoreType.DMA((4,)),
+            pltpu.SemaphoreType.DMA((3,)),
             pltpu.SemaphoreType.DMA,
             pltpu.SemaphoreType.DMA((9,)),
         ],

time: 81.5 us -> 84.1 us (1.032)
  Pallas kernels: 79.9 us -> 82.7 us
    pallas_call x1, Pallas kernels: 79.9 us -> 82.7 us  [body(): pl.pallas_call(kernel, out_shape=pltpu.VMEM(queries.shape, bf16), in_spec...]
where the time goes in v7:
time: 84.1 us; the launch traced here: 84 us
  Pallas kernels  82.7 us (98%)
  local copies, waits for them, and re-layouts  1.32 us (2%)
    pallas_call x1, Pallas kernels, body(): pl.pallas_call(kernel, out_shape=pltpu.VMEM(queries.shape, bf16), in_spec...  82.7 us

profile of v7, /device:TPU:16, one launch (start us, length us, event | category | flops | bytes accessed | tf_op | source)
XLA Modules:
  0.0 84.0 jit_solution(6395171471263898688)
XLA Ops:
  0.0 82.7 %window.1 = bf16[1,2,128,4096]{3,2,1,0:T(8,128)(2,1)S(1)} custom-call(bf16[1,2,128,8192]{3,2,1,0:T(8,128)(2,1)} %tok.1, bf16[1,2,128,4096]{3,2,1,0:T(8,128)(2,1)} %queries.1, bf16[1,8192]{1,0:T(2,128)(2,1)} %gains.1, bf16[1,256,512]{2,1,0:T(8,128)(2,1)} %key_w.1, bf16[1,256,512]{2,1,0:T(8,128)(2,1)} %value_w.1, s32[2,64]{1,0:T(2,128)} %lengths.1), custom_call_target="tpu_custom_call" | custom-call | tf_op jit(solution)/shard_map/window/pallas_call | solution.py:580
  82.7 1.3 %copy.8 = bf16[1,2,128,4096]{3,2,1,0:T(8,128)(2,1)} copy(bf16[1,2,128,4096]{3,2,1,0:T(8,128)(2,1)S(1)} %window.1) | data formatting | bytes 4194304
